TPU v7x, 32 devices: a whole 2x2x4 slice. The times are simulated.
32 devices in a mesh: rep: 2 (over x), dim: 4 (over z), shard: 4 (over y, core).
Axes of the slice: x: 2, y: 2, z: 4, core: 2. Of those that a mesh axis runs over, the one named last changes fastest.
Arguments:
- queries: bfloat16 [16384, 4096], P(('rep', 'shard'), 'dim'), parts along dimension 0
- list_vecs: bfloat16 [1024, 8, 4096], P('shard', None, 'dim')
- list_ids: int32 [1024, 8], P('shard')
- probes: int32 [16384, 8], P(('rep', 'shard')), parts along dimension 0
Outputs:
- output 1: float32 [16384, 10], P(('rep', 'shard')), parts along dimension 0
- output 2: int32 [16384, 10], P(('rep', 'shard')), parts along dimension 0
There are 2 independent parts. A program takes and returns all parts, laid end to end along the dimension named above; an argument that names none is the same for every part.
All inputs are finite; a program needn't handle non-finite values.
Results may differ from a plain program's by a relative error of at most 0.001.
Values are sent between devices in bfloat16 or wider.
A program may use at most 1 GiB of HBM per device.

v0:
```python
import jax
import jax.numpy as jnp
from jax import lax
from jax.sharding import PartitionSpec as P

TOP_K = 10


def slot_capacity(query_rows, num_probes, group_devs):
    pair_total = query_rows * num_probes
    return min(3 * pair_total // 4, 2 * pair_total // group_devs)


def route_slots(probes, lists_dev, group_devs, slot_cap):
    pair_count = probes.shape[0] * probes.shape[1]
    owner_dev = (probes // lists_dev).reshape(pair_count)
    owner_hot = (owner_dev[:, None] == jnp.arange(group_devs, dtype=jnp.int32)[None, :]).astype(jnp.int32)
    earlier = jnp.cumsum(owner_hot, axis=0) - owner_hot
    flat_slot = owner_dev * slot_cap + jnp.sum(earlier * owner_hot, axis=1)
    pair_of_slot = jnp.full((group_devs * slot_cap,), -1, jnp.int32).at[flat_slot].set(jnp.arange(pair_count, dtype=jnp.int32))
    return flat_slot, pair_of_slot


def score_received(list_vecs, recv_rows, recv_list, block_count):
    dim_local = recv_rows.shape[-1]
    row_blocks = recv_rows.reshape(block_count, -1, dim_local)
    list_blocks = recv_list.reshape(block_count, -1)

    def per_block(block_pack):
        block_rows, block_lists = block_pack
        members = list_vecs[jnp.maximum(block_lists, 0)]
        return jnp.einsum('cd,cjd->cj', block_rows, members, preferred_element_type=jnp.float32)

    block_scores = lax.map(per_block, (row_blocks, list_blocks))
    return block_scores.reshape(recv_list.shape + (list_vecs.shape[1],))


def best_first(neg_keys, cand_ids, keep_count):
    key_sorted, ids_sorted = lax.sort((neg_keys, cand_ids), dimension=neg_keys.ndim - 1, num_keys=2)
    return key_sorted[..., :keep_count], ids_sorted[..., :keep_count]


def solution(mesh):
    group_devs = mesh.shape['shard']
    dim_devs = mesh.shape['dim']
    row_spec = P(('rep', 'shard'), None)

    def local_search(queries, list_vecs, list_ids, probes):
        query_rows, num_probes = probes.shape
        lists_dev, list_len, dim_local = list_vecs.shape
        slot_cap = slot_capacity(query_rows, num_probes, group_devs)
        slot_share = slot_cap // dim_devs
        keep_list = min(TOP_K, list_len)
        flat_slot, pair_of_slot = route_slots(probes, lists_dev, group_devs, slot_cap)
        pair_index = jnp.maximum(pair_of_slot, 0)
        send_rows = queries[pair_index // num_probes].reshape(group_devs, slot_cap, dim_local)
        send_list = jnp.where(pair_of_slot >= 0, probes.reshape(-1)[pair_index] % lists_dev, -1).reshape(group_devs, slot_cap)
        recv_rows = lax.all_to_all(send_rows, 'shard', 0, 0)
        recv_list = lax.all_to_all(send_list, 'shard', 0, 0)
        partial = score_received(list_vecs, recv_rows, recv_list, group_devs * dim_devs)
        scores = lax.psum_scatter(partial, 'dim', scatter_dimension=1, tiled=True)
        my_list = lax.dynamic_index_in_dim(recv_list.reshape(group_devs, dim_devs, slot_share), lax.axis_index('dim'), axis=1, keepdims=False)
        member_ids = list_ids[jnp.maximum(my_list, 0)]
        is_member = (member_ids >= 0) & (my_list >= 0)[:, :, None]
        best_keys, best_ids = best_first(jnp.where(is_member, -scores, jnp.inf), member_ids, keep_list)
        back_keys = lax.all_to_all(best_keys, 'shard', 0, 0)
        back_ids = lax.all_to_all(best_ids, 'shard', 0, 0)
        slot_keys = lax.all_gather(back_keys, 'dim', axis=1, tiled=True).reshape(group_devs * slot_cap, keep_list)
        slot_ids = lax.all_gather(back_ids, 'dim', axis=1, tiled=True).reshape(group_devs * slot_cap, keep_list)
        cand_keys = slot_keys[flat_slot].reshape(query_rows, num_probes * keep_list)
        cand_ids = slot_ids[flat_slot].reshape(query_rows, num_probes * keep_list)
        top_keys, top_ids = best_first(cand_keys, cand_ids, TOP_K)
        return -top_keys, top_ids

    return jax.shard_map(local_search, mesh=mesh,
                         in_specs=(P(('rep', 'shard'), 'dim'), P('shard', None, 'dim'), P('shard', None), row_spec),
                         out_specs=(row_spec, row_spec), check_vma=False)
```

profile of v0, /device:TPU:0, one launch (start us, length us, event | category | flops | bytes accessed | tf_op | source)
XLA Modules:
  0.0 2548.8 jit_solution(1231897219108986939)
XLA Ops:
  13.4 60.4 %scatter_custom_fusion = s32[32768]{0:T(1024)S(1)} fusion(s32[16384]{0:T(1024)S(1)} %bitcast.56, s32[16384]{0:T(1024)S(1)} %iota.17, s32[]{:T(128)} %constant.108.clone.1), kind=kCustom, calls=%fused_computation.42 | custom fusion | bytes 131076 | tf_op jit(solution)/shard_map/scatter | solution.py:20
  74.3 180.5 %gather_fusion.1 = s32[32768]{0:T(1024)S(1)} fusion(s32[16384]{0:T(1024)S(1)} %reshape.118, s32[32768]{0:T(1024)S(1)} %maximum_clamp_fusion), kind=kCustom, calls=%fused_computation.1 | custom fusion | bytes 393216 | tf_op jit(solution)/shard_map/gather | solution.py:57
  255.7 4.3 all-to-all-start
  260.0 161.9 %gather_fusion.3 = bf16[32768,1024]{1,0:T(8,128)(2,1)} fusion(bf16[2048,1024]{1,0:T(8,128)(2,1)} %param.6, s32[32768]{0:T(1024)S(1)} %get-tuple-element.53), kind=kCustom, calls=%fused_computation.3 | custom fusion | bytes 134348800 | tf_op jit(solution)/shard_map/gather | solution.py:56
  421.9 13.0 all-to-all-start.1
  436.5 720.8 %all-to-all-done.1 = bf16[4,8192,1024]{2,1,0:T(8,128)(2,1)} async-done(((bf16[4,8192,1024]{2,1,0:T(8,128)(2,1)}), bf16[4,8192,1024]{2,1,0:T(8,128)(2,1)}, u32[]{:S(2)}, u32[]{:S(2)}) %all-to-all-start.1) | async-done | bytes 67108896 | tf_op jit(solution)/shard_map/all_to_all | solution.py:58
  1157.2 1146.1 %while.10 = (s32[]{:T(128)}, f32[16,2048,8]{1,2,0:T(8,128)}, bf16[16,2048,1024]{2,1,0:T(8,128)(2,1)}, s32[16,2048]{1,0:T(8,128)S(1)}, bf16[256,8,1024]{2,1,0:T(8,128)(2,1)}, /*index=5*/s32[]{:T(128)}) while((s32[]{:T(128)}, f32[16,2048,8]{1,2,0:T(8,128)}, bf16[16,2048,1024]{2,1,0:T(8,128)(2,1)}, s32[16,2048]{1,0:T(8,128)S(1)}, ...), condition=%wide.region_5.6_spmd, body=%wide.region_4.5_spmd.sunk | while | flops 33558528 | bytes 113615432 | solution.py:34
  1157.3 26.5 %gather_fusion = bf16[2048,8,1024]{2,1,0:T(8,128)(2,1)} fusion(bf16[256,8,1024]{2,1,0:T(8,128)(2,1)} %get-tuple-element.103, s32[2048]{0:T(1024)S(1)} %broadcast_clamp_fusion.4), kind=kCustom, calls=%fused_computation.clone.1 | custom fusion | bytes 67117056 | tf_op jit(solution)/shard_map/while/body/eval_jaxpr/gather | solution.py:31
  1183.8 2.6 dynamic-slice_bitcast_fusion.2
  1186.4 41.3 %fusion.20 = f32[2048,1,8]{2,1,0:T(1,128)S(1)} fusion(bf16[2048,8,1024]{2,1,0:T(8,128)(2,1)} %gather_fusion, bf16[2048,1024,1]{1,0,2:T(8,128)(2,1)S(1)} %dynamic-slice_bitcast_fusion.2), kind=kOutput, calls=%fused_computation.7.clone.1 | convolution fusion | flops 33554432 | bytes 37814272 | tf_op jit(solution)/shard_map/while/body/eval_jaxpr/cd,cjd->cj/dot_general | solution.py:32
  1228.9 26.5 %gather_fusion = bf16[2048,8,1024]{2,1,0:T(8,128)(2,1)} fusion(bf16[256,8,1024]{2,1,0:T(8,128)(2,1)} %get-tuple-element.103, s32[2048]{0:T(1024)S(1)} %broadcast_clamp_fusion.4), kind=kCustom, calls=%fused_computation.clone.1 | custom fusion | bytes 67117056 | tf_op jit(solution)/shard_map/while/body/eval_jaxpr/gather | solution.py:31
  1255.4 2.6 dynamic-slice_bitcast_fusion.2
  1258.0 41.3 %fusion.20 = f32[2048,1,8]{2,1,0:T(1,128)S(1)} fusion(bf16[2048,8,1024]{2,1,0:T(8,128)(2,1)} %gather_fusion, bf16[2048,1024,1]{1,0,2:T(8,128)(2,1)S(1)} %dynamic-slice_bitcast_fusion.2), kind=kOutput, calls=%fused_computation.7.clone.1 | convolution fusion | flops 33554432 | bytes 37814272 | tf_op jit(solution)/shard_map/while/body/eval_jaxpr/cd,cjd->cj/dot_general | solution.py:32
  1300.5 26.5 %gather_fusion = bf16[2048,8,1024]{2,1,0:T(8,128)(2,1)} fusion(bf16[256,8,1024]{2,1,0:T(8,128)(2,1)} %get-tuple-element.103, s32[2048]{0:T(1024)S(1)} %broadcast_clamp_fusion.4), kind=kCustom, calls=%fused_computation.clone.1 | custom fusion | bytes 67117056 | tf_op jit(solution)/shard_map/while/body/eval_jaxpr/gather | solution.py:31
  1327.0 2.6 dynamic-slice_bitcast_fusion.2
  1329.7 41.3 %fusion.20 = f32[2048,1,8]{2,1,0:T(1,128)S(1)} fusion(bf16[2048,8,1024]{2,1,0:T(8,128)(2,1)} %gather_fusion, bf16[2048,1024,1]{1,0,2:T(8,128)(2,1)S(1)} %dynamic-slice_bitcast_fusion.2), kind=kOutput, calls=%fused_computation.7.clone.1 | convolution fusion | flops 33554432 | bytes 37814272 | tf_op jit(solution)/shard_map/while/body/eval_jaxpr/cd,cjd->cj/dot_general | solution.py:32
  1372.2 26.5 %gather_fusion = bf16[2048,8,1024]{2,1,0:T(8,128)(2,1)} fusion(bf16[256,8,1024]{2,1,0:T(8,128)(2,1)} %get-tuple-element.103, s32[2048]{0:T(1024)S(1)} %broadcast_clamp_fusion.4), kind=kCustom, calls=%fused_computation.clone.1 | custom fusion | bytes 67117056 | tf_op jit(solution)/shard_map/while/body/eval_jaxpr/gather | solution.py:31
  1398.7 2.6 dynamic-slice_bitcast_fusion.2
  1401.3 41.3 %fusion.20 = f32[2048,1,8]{2,1,0:T(1,128)S(1)} fusion(bf16[2048,8,1024]{2,1,0:T(8,128)(2,1)} %gather_fusion, bf16[2048,1024,1]{1,0,2:T(8,128)(2,1)S(1)} %dynamic-slice_bitcast_fusion.2), kind=kOutput, calls=%fused_computation.7.clone.1 | convolution fusion | flops 33554432 | bytes 37814272 | tf_op jit(solution)/shard_map/while/body/eval_jaxpr/cd,cjd->cj/dot_general | solution.py:32
  1443.8 26.5 %gather_fusion = bf16[2048,8,1024]{2,1,0:T(8,128)(2,1)} fusion(bf16[256,8,1024]{2,1,0:T(8,128)(2,1)} %get-tuple-element.103, s32[2048]{0:T(1024)S(1)} %broadcast_clamp_fusion.4), kind=kCustom, calls=%fused_computation.clone.1 | custom fusion | bytes 67117056 | tf_op jit(solution)/shard_map/while/body/eval_jaxpr/gather | solution.py:31
  1470.3 2.6 dynamic-slice_bitcast_fusion.2
  1472.9 41.3 %fusion.20 = f32[2048,1,8]{2,1,0:T(1,128)S(1)} fusion(bf16[2048,8,1024]{2,1,0:T(8,128)(2,1)} %gather_fusion, bf16[2048,1024,1]{1,0,2:T(8,128)(2,1)S(1)} %dynamic-slice_bitcast_fusion.2), kind=kOutput, calls=%fused_computation.7.clone.1 | convolution fusion | flops 33554432 | bytes 37814272 | tf_op jit(solution)/shard_map/while/body/eval_jaxpr/cd,cjd->cj/dot_general | solution.py:32
  1515.4 26.5 %gather_fusion = bf16[2048,8,1024]{2,1,0:T(8,128)(2,1)} fusion(bf16[256,8,1024]{2,1,0:T(8,128)(2,1)} %get-tuple-element.103, s32[2048]{0:T(1024)S(1)} %broadcast_clamp_fusion.4), kind=kCustom, calls=%fused_computation.clone.1 | custom fusion | bytes 67117056 | tf_op jit(solution)/shard_map/while/body/eval_jaxpr/gather | solution.py:31
  1541.9 2.6 dynamic-slice_bitcast_fusion.2
  1544.6 41.3 %fusion.20 = f32[2048,1,8]{2,1,0:T(1,128)S(1)} fusion(bf16[2048,8,1024]{2,1,0:T(8,128)(2,1)} %gather_fusion, bf16[2048,1024,1]{1,0,2:T(8,128)(2,1)S(1)} %dynamic-slice_bitcast_fusion.2), kind=kOutput, calls=%fused_computation.7.clone.1 | convolution fusion | flops 33554432 | bytes 37814272 | tf_op jit(solution)/shard_map/while/body/eval_jaxpr/cd,cjd->cj/dot_general | solution.py:32
  1587.1 26.5 %gather_fusion = bf16[2048,8,1024]{2,1,0:T(8,128)(2,1)} fusion(bf16[256,8,1024]{2,1,0:T(8,128)(2,1)} %get-tuple-element.103, s32[2048]{0:T(1024)S(1)} %broadcast_clamp_fusion.4), kind=kCustom, calls=%fused_computation.clone.1 | custom fusion | bytes 67117056 | tf_op jit(solution)/shard_map/while/body/eval_jaxpr/gather | solution.py:31
  1613.6 2.6 dynamic-slice_bitcast_fusion.2
  1616.2 41.3 %fusion.20 = f32[2048,1,8]{2,1,0:T(1,128)S(1)} fusion(bf16[2048,8,1024]{2,1,0:T(8,128)(2,1)} %gather_fusion, bf16[2048,1024,1]{1,0,2:T(8,128)(2,1)S(1)} %dynamic-slice_bitcast_fusion.2), kind=kOutput, calls=%fused_computation.7.clone.1 | convolution fusion | flops 33554432 | bytes 37814272 | tf_op jit(solution)/shard_map/while/body/eval_jaxpr/cd,cjd->cj/dot_general | solution.py:32
  1658.7 26.5 %gather_fusion = bf16[2048,8,1024]{2,1,0:T(8,128)(2,1)} fusion(bf16[256,8,1024]{2,1,0:T(8,128)(2,1)} %get-tuple-element.103, s32[2048]{0:T(1024)S(1)} %broadcast_clamp_fusion.4), kind=kCustom, calls=%fused_computation.clone.1 | custom fusion | bytes 67117056 | tf_op jit(solution)/shard_map/while/body/eval_jaxpr/gather | solution.py:31
  1685.2 2.6 dynamic-slice_bitcast_fusion.2
  1687.8 41.3 %fusion.20 = f32[2048,1,8]{2,1,0:T(1,128)S(1)} fusion(bf16[2048,8,1024]{2,1,0:T(8,128)(2,1)} %gather_fusion, bf16[2048,1024,1]{1,0,2:T(8,128)(2,1)S(1)} %dynamic-slice_bitcast_fusion.2), kind=kOutput, calls=%fused_computation.7.clone.1 | convolution fusion | flops 33554432 | bytes 37814272 | tf_op jit(solution)/shard_map/while/body/eval_jaxpr/cd,cjd->cj/dot_general | solution.py:32
  1730.3 26.5 %gather_fusion = bf16[2048,8,1024]{2,1,0:T(8,128)(2,1)} fusion(bf16[256,8,1024]{2,1,0:T(8,128)(2,1)} %get-tuple-element.103, s32[2048]{0:T(1024)S(1)} %broadcast_clamp_fusion.4), kind=kCustom, calls=%fused_computation.clone.1 | custom fusion | bytes 67117056 | tf_op jit(solution)/shard_map/while/body/eval_jaxpr/gather | solution.py:31
  1759.4 41.3 %fusion.20 = f32[2048,1,8]{2,1,0:T(1,128)S(1)} fusion(bf16[2048,8,1024]{2,1,0:T(8,128)(2,1)} %gather_fusion, bf16[2048,1024,1]{1,0,2:T(8,128)(2,1)S(1)} %dynamic-slice_bitcast_fusion.2), kind=kOutput, calls=%fused_computation.7.clone.1 | convolution fusion | flops 33554432 | bytes 37814272 | tf_op jit(solution)/shard_map/while/body/eval_jaxpr/cd,cjd->cj/dot_general | solution.py:32
  1801.9 26.5 %gather_fusion = bf16[2048,8,1024]{2,1,0:T(8,128)(2,1)} fusion(bf16[256,8,1024]{2,1,0:T(8,128)(2,1)} %get-tuple-element.103, s32[2048]{0:T(1024)S(1)} %broadcast_clamp_fusion.4), kind=kCustom, calls=%fused_computation.clone.1 | custom fusion | bytes 67117056 | tf_op jit(solution)/shard_map/while/body/eval_jaxpr/gather | solution.py:31
  1828.4 2.6 dynamic-slice_bitcast_fusion.2
  1831.1 41.3 %fusion.20 = f32[2048,1,8]{2,1,0:T(1,128)S(1)} fusion(bf16[2048,8,1024]{2,1,0:T(8,128)(2,1)} %gather_fusion, bf16[2048,1024,1]{1,0,2:T(8,128)(2,1)S(1)} %dynamic-slice_bitcast_fusion.2), kind=kOutput, calls=%fused_computation.7.clone.1 | convolution fusion | flops 33554432 | bytes 37814272 | tf_op jit(solution)/shard_map/while/body/eval_jaxpr/cd,cjd->cj/dot_general | solution.py:32
  1873.6 26.5 %gather_fusion = bf16[2048,8,1024]{2,1,0:T(8,128)(2,1)} fusion(bf16[256,8,1024]{2,1,0:T(8,128)(2,1)} %get-tuple-element.103, s32[2048]{0:T(1024)S(1)} %broadcast_clamp_fusion.4), kind=kCustom, calls=%fused_computation.clone.1 | custom fusion | bytes 67117056 | tf_op jit(solution)/shard_map/while/body/eval_jaxpr/gather | solution.py:31
  1902.7 41.3 %fusion.20 = f32[2048,1,8]{2,1,0:T(1,128)S(1)} fusion(bf16[2048,8,1024]{2,1,0:T(8,128)(2,1)} %gather_fusion, bf16[2048,1024,1]{1,0,2:T(8,128)(2,1)S(1)} %dynamic-slice_bitcast_fusion.2), kind=kOutput, calls=%fused_computation.7.clone.1 | convolution fusion | flops 33554432 | bytes 37814272 | tf_op jit(solution)/shard_map/while/body/eval_jaxpr/cd,cjd->cj/dot_general | solution.py:32
  1945.2 26.5 %gather_fusion = bf16[2048,8,1024]{2,1,0:T(8,128)(2,1)} fusion(bf16[256,8,1024]{2,1,0:T(8,128)(2,1)} %get-tuple-element.103, s32[2048]{0:T(1024)S(1)} %broadcast_clamp_fusion.4), kind=kCustom, calls=%fused_computation.clone.1 | custom fusion | bytes 67117056 | tf_op jit(solution)/shard_map/while/body/eval_jaxpr/gather | solution.py:31
  1971.7 2.6 dynamic-slice_bitcast_fusion.2
  1974.3 41.3 %fusion.20 = f32[2048,1,8]{2,1,0:T(1,128)S(1)} fusion(bf16[2048,8,1024]{2,1,0:T(8,128)(2,1)} %gather_fusion, bf16[2048,1024,1]{1,0,2:T(8,128)(2,1)S(1)} %dynamic-slice_bitcast_fusion.2), kind=kOutput, calls=%fused_computation.7.clone.1 | convolution fusion | flops 33554432 | bytes 37814272 | tf_op jit(solution)/shard_map/while/body/eval_jaxpr/cd,cjd->cj/dot_general | solution.py:32
  2016.8 26.5 %gather_fusion = bf16[2048,8,1024]{2,1,0:T(8,128)(2,1)} fusion(bf16[256,8,1024]{2,1,0:T(8,128)(2,1)} %get-tuple-element.103, s32[2048]{0:T(1024)S(1)} %broadcast_clamp_fusion.4), kind=kCustom, calls=%fused_computation.clone.1 | custom fusion | bytes 67117056 | tf_op jit(solution)/shard_map/while/body/eval_jaxpr/gather | solution.py:31
  2043.3 2.6 dynamic-slice_bitcast_fusion.2
  2046.0 41.3 %fusion.20 = f32[2048,1,8]{2,1,0:T(1,128)S(1)} fusion(bf16[2048,8,1024]{2,1,0:T(8,128)(2,1)} %gather_fusion, bf16[2048,1024,1]{1,0,2:T(8,128)(2,1)S(1)} %dynamic-slice_bitcast_fusion.2), kind=kOutput, calls=%fused_computation.7.clone.1 | convolution fusion | flops 33554432 | bytes 37814272 | tf_op jit(solution)/shard_map/while/body/eval_jaxpr/cd,cjd->cj/dot_general | solution.py:32
  2088.4 26.5 %gather_fusion = bf16[2048,8,1024]{2,1,0:T(8,128)(2,1)} fusion(bf16[256,8,1024]{2,1,0:T(8,128)(2,1)} %get-tuple-element.103, s32[2048]{0:T(1024)S(1)} %broadcast_clamp_fusion.4), kind=kCustom, calls=%fused_computation.clone.1 | custom fusion | bytes 67117056 | tf_op jit(solution)/shard_map/while/body/eval_jaxpr/gather | solution.py:31
  2114.9 2.6 dynamic-slice_bitcast_fusion.2
  2117.6 41.3 %fusion.20 = f32[2048,1,8]{2,1,0:T(1,128)S(1)} fusion(bf16[2048,8,1024]{2,1,0:T(8,128)(2,1)} %gather_fusion, bf16[2048,1024,1]{1,0,2:T(8,128)(2,1)S(1)} %dynamic-slice_bitcast_fusion.2), kind=kOutput, calls=%fused_computation.7.clone.1 | convolution fusion | flops 33554432 | bytes 37814272 | tf_op jit(solution)/shard_map/while/body/eval_jaxpr/cd,cjd->cj/dot_general | solution.py:32
  2160.1 26.5 %gather_fusion = bf16[2048,8,1024]{2,1,0:T(8,128)(2,1)} fusion(bf16[256,8,1024]{2,1,0:T(8,128)(2,1)} %get-tuple-element.103, s32[2048]{0:T(1024)S(1)} %broadcast_clamp_fusion.4), kind=kCustom, calls=%fused_computation.clone.1 | custom fusion | bytes 67117056 | tf_op jit(solution)/shard_map/while/body/eval_jaxpr/gather | solution.py:31
  2189.2 41.3 %fusion.20 = f32[2048,1,8]{2,1,0:T(1,128)S(1)} fusion(bf16[2048,8,1024]{2,1,0:T(8,128)(2,1)} %gather_fusion, bf16[2048,1024,1]{1,0,2:T(8,128)(2,1)S(1)} %dynamic-slice_bitcast_fusion.2), kind=kOutput, calls=%fused_computation.7.clone.1 | convolution fusion | flops 33554432 | bytes 37814272 | tf_op jit(solution)/shard_map/while/body/eval_jaxpr/cd,cjd->cj/dot_general | solution.py:32
  2231.7 26.5 %gather_fusion = bf16[2048,8,1024]{2,1,0:T(8,128)(2,1)} fusion(bf16[256,8,1024]{2,1,0:T(8,128)(2,1)} %get-tuple-element.103, s32[2048]{0:T(1024)S(1)} %broadcast_clamp_fusion.4), kind=kCustom, calls=%fused_computation.clone.1 | custom fusion | bytes 67117056 | tf_op jit(solution)/shard_map/while/body/eval_jaxpr/gather | solution.py:31
  2260.8 41.3 %fusion.20 = f32[2048,1,8]{2,1,0:T(1,128)S(1)} fusion(bf16[2048,8,1024]{2,1,0:T(8,128)(2,1)} %gather_fusion, bf16[2048,1024,1]{1,0,2:T(8,128)(2,1)S(1)} %dynamic-slice_bitcast_fusion.2), kind=kOutput, calls=%fused_computation.7.clone.1 | convolution fusion | flops 33554432 | bytes 37814272 | tf_op jit(solution)/shard_map/while/body/eval_jaxpr/cd,cjd->cj/dot_general | solution.py:32
  2304.7 27.7 %gather_fusion.2 = s32[8192,8]{1,0:T(8,128)} fusion(s32[256,8]{1,0:T(8,128)S(1)} %copy.28, s32[8192]{0:T(1024)S(1)} %broadcast_clamp_fusion.2), kind=kCustom, calls=%fused_computation.2 | custom fusion | bytes 557056 | tf_op jit(solution)/shard_map/gather | solution.py:63
  2332.4 2.8 copy.29
  2336.3 2.9 sort.46
  2339.2 8.9 all_to_all.24
  2348.2 9.0 all_to_all.25
  2357.2 20.1 all-gather.5.cloned.1.call-done
  2377.3 9.1 copy.32
  2386.5 60.2 %gather_fusion.5 = s32[16384,8]{1,0:T(8,128)} fusion(s32[32768,8]{1,0:T(8,128)} %bitcast.51, s32[16384]{0:T(1024)S(1)} %broadcast_clamp_fusion.1), kind=kCustom, calls=%fused_computation.5 | custom fusion | bytes 1114112 | tf_op jit(solution)/shard_map/gather | solution.py:71
  2446.7 5.6 reshape.127
  2452.6 9.2 copy.31
  2461.7 60.2 %gather_fusion.4 = f32[16384,8]{1,0:T(8,128)} fusion(f32[32768,8]{1,0:T(8,128)} %bitcast.50, s32[16384]{0:T(1024)S(1)} %broadcast_clamp_fusion.1), kind=kCustom, calls=%fused_computation.4 | custom fusion | bytes 1114112 | tf_op jit(solution)/shard_map/gather | solution.py:70
  2521.9 5.6 reshape.125
  2527.9 13.1 sort.47
  (124 shorter events, 42.3 us)
Async XLA Ops:
  12.8 0.6 copy-start.1
  255.7 166.2 %all-to-all-start = ((s32[4,1,8192]{2,1,0:T(1,128)}), s32[4,1,8192]{2,1,0:T(1,128)}, u32[]{:S(2)}, u32[]{:S(2)}) async-start(s32[4,1,8192]{2,1,0:T(1,128)} %bitcast.9), calls=%async_computation | async-start | bytes 262144 | tf_op jit(solution)/shard_map/all_to_all | solution.py:59
  421.9 735.4 %all-to-all-start.1 = ((bf16[4,8192,1024]{2,1,0:T(8,128)(2,1)}), bf16[4,8192,1024]{2,1,0:T(8,128)(2,1)}, u32[]{:S(2)}, u32[]{:S(2)}) async-start(bf16[4,8192,1024]{2,1,0:T(8,128)(2,1)} %bitcast.12), calls=%async_computation.1 | async-start | bytes 134217728 | tf_op jit(solution)/shard_map/all_to_all | solution.py:58
  434.9 1900.3 %reduce-scatter.2.cloned.1.call-start = ((), (), s32[]{:S(2)}) async-start(), calls=%async_computation.5 | async-start | bytes 1310720 | tf_op jit(solution)/shard_map/reduce_scatter | solution.py:61
  436.4 720.9 %copy-start = (s32[4,8192]{1,0:T(4,128)}, s32[4,8192]{1,0:T(4,128)S(1)}, u32[]{:S(2)}) copy-start(s32[4,8192]{1,0:T(4,128)S(1)} %reduce) | copy-start | bytes 393220
  1157.2 1146.1 %copy-start.3 = (s32[256,8]{0,1:T(8,128)S(1)}, s32[256,8]{0,1:T(8,128)}, u32[]{:S(2)}) copy-start(s32[256,8]{0,1:T(8,128)} %param.8) | copy-start | bytes 24580
  2303.3 74.0 %all-gather.5.cloned.1.call-start = ((), (), s32[]{:S(2)}) async-start(), calls=%async_computation.7 | async-start | bytes 1310720 | tf_op jit(solution)/shard_map/all_gather | solution.py:69
  2304.7 52.5 %copy-start.2 = (s32[16384,1]{0,1:T(1,128)S(1)}, s32[16384,1]{0,1:T(1,128)}, u32[]{:S(2)}) copy-start(s32[16384,1]{0,1:T(1,128)} %copy-done.1) | copy-start | bytes 196612
  2348.2 104.4 %all-gather.3.cloned.1.call-start = ((), (), s32[]{:S(2)}) async-start(), calls=%async_computation.6 | async-start | bytes 1310720 | tf_op jit(solution)/shard_map/all_gather | solution.py:68
Sparse Core Ops, SparseCore 0:
  2303.4 28.3 reduce-scatter.1
  2348.3 28.9 all-gather.4
  2378.9 27.2 all-gather.2
where the time goes:
time: 2550 us
  local copies, waits for them, and re-layouts  1070 us (42%)
  waiting for transfers between devices  741 us (29%)
  matrix products  661 us (26%)
    all_to_all x1, waiting for transfers between devices, local_search(): recv_rows = lax.all_to_all(send_rows, 'shard', 0, 0)  721 us
    dot_general x16, matrix products, per_block(): jnp.einsum('cd,cjd->cj', block_rows, members, preferred_element_type=jnp....  661 us
    gather x16, local copies, waits for them, and re-layouts, per_block(): members = list_vecs[jnp.maximum(block_lists, 0)]  424 us
    gather x1, local copies, waits for them, and re-layouts, local_search(): probes.reshape(-1)[pair_index] % lists_dev  181 us
    gather x1, local copies, waits for them, and re-layouts, local_search(): queries[pair_index // num_probes].reshape(group_devs, slot_cap, dim_local)  162 us
    scatter x1, local copies, waits for them, and re-layouts, route_slots(): jnp.full((group_devs * slot_cap,), -1, jnp.int32).at[flat_slot]  60.4 us
    gather x1, local copies, waits for them, and re-layouts, local_search(): cand_ids = slot_ids[flat_slot].reshape(query_rows, num_probes * keep_list)  60.2 us
    gather x1, local copies, waits for them, and re-layouts, local_search(): cand_keys = slot_keys[flat_slot].reshape(query_rows, num_probes * keep_list)  60.2 us
  transfers between devices with their start and end apart: 5, of which 2 were waited for; matrix products, arithmetic and copies ran while one was open for 11% of the time, Pallas kernels for 0%

commit v1 on v0

v1 whole, which is shorter than its diff:
```python
import functools

import jax
import jax.numpy as jnp
from jax import lax
from jax.experimental import pallas as pl
from jax.experimental.pallas import tpu as pltpu
from jax.sharding import PartitionSpec as P

TOP_K = 10
LIST_LEN = 8
GROUP_LISTS = 8
GROUP_ROWS = GROUP_LISTS * LIST_LEN
STEP_GROUPS = 4
STEP_ROWS = STEP_GROUPS * GROUP_ROWS
LANES = 128
MESH = pl.DeviceIdType.MESH
BIG = 1e9


def flip(index, bit):
    return index + bit - 2 * bit * ((index // bit) % 2)


def search_kernel(dims, q_hbm, l_hbm, probes_ref, ids_ref, out_s, out_i,
                  raw, qv, vecs, perm, acc, parts, ids_all, cand_ids, res,
                  load_l, load_q, send_o, recv_o, send_y, recv_y, send_x, recv_x,
                  send_dy, recv_dy, send_dx, recv_dx, send_i, recv_i,
                  send_r, recv_r, send_g, recv_g):
    rows_q = qv.shape[0]
    lists_dev = ids_ref.shape[1]
    block_rows = lists_dev * LIST_LEN
    block_groups = lists_dev // GROUP_LISTS
    chunks = block_groups // 2
    block_steps = block_groups // STEP_GROUPS
    width = rows_q // dims
    x, z, s = lax.axis_index('rep'), lax.axis_index('dim'), lax.axis_index('shard')
    twin, across, far = flip(s, 1), flip(s, 2), flip(flip(s, 1), 2)
    other_x = 1 - x

    def at(**place):
        return {'rep': x, 'dim': z, 'shard': s, **place}

    def group_rows(group):
        return pl.ds(pl.multiple_of(group * GROUP_ROWS, GROUP_ROWS), GROUP_ROWS)

    def step_rows(step):
        return pl.ds(pl.multiple_of(step * STEP_ROWS, STEP_ROWS), STEP_ROWS)

    def remote(src, dst, send, recv, device):
        return pltpu.make_async_remote_copy(src_ref=src, dst_ref=dst, send_sem=send, recv_sem=recv,
                                            device_id=device, device_id_type=MESH)

    def load_list(block):
        return pltpu.make_async_copy(l_hbm.at[step_rows(block)], raw.at[step_rows(block)], load_l.at[block])

    def load_query(part):
        rows = pl.ds(pl.multiple_of(part * width, width), width)
        return pltpu.make_async_copy(q_hbm.at[rows], qv.at[rows], load_q.at[part])

    def own_copy(block):
        return remote(vecs.at[step_rows(block)], vecs.at[step_rows(block_steps + block)],
                      send_o.at[block], recv_o.at[block], at(shard=twin))

    def slot(chunk, which):
        return vecs.at[group_rows(2 * block_groups + STEP_GROUPS * chunk + which)]

    def y_copy(chunk):
        return remote(vecs.at[group_rows(chunks * x + chunk)], slot(chunk, 0), send_y.at[chunk], recv_y.at[chunk], at(shard=across))

    def x_copy(chunk):
        return remote(slot(chunk, 0), slot(chunk, 1), send_x.at[chunk], recv_x.at[chunk], at(rep=other_x))

    def dy_copy(chunk):
        return remote(slot(chunk, 0), slot(chunk, 2), send_dy.at[chunk], recv_dy.at[chunk], at(shard=twin))

    def dx_copy(chunk):
        return remote(slot(chunk, 1), slot(chunk, 3), send_dx.at[chunk], recv_dx.at[chunk], at(shard=twin))

    def id_copy(which, peer):
        return remote(ids_ref, ids_all.at[s], send_i.at[which], recv_i.at[which], at(shard=peer))

    def peer_slot(source, target):
        return (source - target - 1 + dims) % dims

    def part_copy(target, which):
        return remote(acc.at[target], parts.at[peer_slot(z, target)], send_r.at[which], recv_r.at[peer_slot(z, target)], at(dim=target))

    def res_copy(target, which):
        return remote(res.at[z], res.at[z], send_g.at[which], recv_g.at[peer_slot(z, target)], at(dim=target))

    def target_at(turn):
        if dims == 1:
            return 0
        half = dims // 2
        low = z // half == 0
        ahead = turn
        far_target = jnp.where(low, dims - 1 - ahead, ahead)
        near = turn - half
        base = jnp.where(low, 0, half)
        near_target = base + (z - base + 1 + near) % half
        return jnp.where(turn < half, far_target, near_target)

    def block_at(turn):
        return (block_steps // 2 * x + turn) % block_steps

    for turn in range(block_steps):
        load_list(block_at(turn)).start()
    for part in range(dims):
        load_query(part).start()

    barrier = pltpu.get_barrier_semaphore()
    peers = [at(shard=twin), at(shard=across), at(shard=far), at(rep=other_x)]
    peers += [at(dim=(z + hop) % dims) for hop in range(1, dims)]
    for peer in peers:
        pl.semaphore_signal(barrier, inc=1, device_id=peer, device_id_type=MESH)

    row = lax.broadcasted_iota(jnp.int32, (STEP_ROWS, STEP_ROWS), 0)
    col = lax.broadcasted_iota(jnp.int32, (STEP_ROWS, STEP_ROWS), 1)
    source = (row // GROUP_ROWS) * GROUP_ROWS + (row % GROUP_LISTS) * LIST_LEN + (row // GROUP_LISTS) % LIST_LEN
    perm[...] = jnp.where(col == source, 1.0, 0.0).astype(jnp.bfloat16)
    acc[...] = jnp.zeros_like(acc)
    ids_all[s] = ids_ref[...]

    pl.semaphore_wait(barrier, len(peers))
    for which, peer in enumerate((twin, across, far)):
        id_copy(which, peer).start()

    def send_block(turn):
        own_copy(block_at(turn)).start()

        @pl.when(turn < block_steps // 2)
        def _():
            for sub in range(STEP_GROUPS):
                y_copy(STEP_GROUPS * turn + sub).start()

    def arrange(turn, carry):
        block = block_at(turn)
        load_list(block).wait()
        moved = jnp.dot(perm[...], raw[step_rows(block), :], preferred_element_type=jnp.float32)
        vecs[step_rows(block), :] = moved.astype(jnp.bfloat16)

        @pl.when(turn > 0)
        def _():
            send_block(turn - 1)
        return carry

    lax.fori_loop(0, block_steps, arrange, 0)

    for part in range(dims):
        load_query(part).wait()
    for which, peer in enumerate((twin, across, far)):
        remote(ids_ref, ids_all.at[peer], send_i.at[which], recv_i.at[which], at(shard=peer)).wait_recv()

    def name_candidates(tile, carry):
        cols = pl.ds(pl.multiple_of(z * width + tile * LANES, LANES), LANES)
        probe = probes_ref[:, cols]
        lane, page = probe % LANES, probe // LANES
        pages = lists_dev // LANES
        for member in range(LIST_LEN):
            got = jnp.zeros((probe.shape[0], LANES), jnp.int32)
            for number in range(4 * pages):
                table = ids_all[number // pages, member:member + 1, (number % pages) * LANES:(number % pages + 1) * LANES]
                table = jnp.broadcast_to(table, (probe.shape[0], LANES))
                picked = jnp.take_along_axis(table, lane, axis=1, mode='promise_in_bounds')
                got = jnp.where(page == number, picked, got)
            cand_ids[member, :, pl.ds(pl.multiple_of(tile * LANES, LANES), LANES)] = got.astype(jnp.float32)
        return carry

    lax.fori_loop(0, width // LANES, name_candidates, 0)
    send_block(block_steps - 1)

    def score(step, heads, part):
        lists = vecs[step_rows(step), :]
        rows = pl.ds(pl.multiple_of(part * width, width), width)
        scores = lax.dot_general(lists, qv[rows, :], (((1,), (1,)), ((), ())), preferred_element_type=jnp.float32)
        for tile in range(width // LANES):
            probe = probes_ref[:, pl.ds(pl.multiple_of(part * width + tile * LANES, LANES), LANES)]
            low, head = probe % GROUP_LISTS, probe // GROUP_LISTS
            hits = [head == want for want in heads]
            lanes = slice(tile * LANES, (tile + 1) * LANES)
            for member in range(LIST_LEN):
                kept = acc[part, member, :, lanes]
                for group, hit in enumerate(hits):
                    first = group * GROUP_ROWS + member * GROUP_LISTS
                    picked = jnp.take_along_axis(scores[first:first + GROUP_LISTS, lanes], low, axis=0, mode='promise_in_bounds')
                    kept = jnp.where(hit, picked, kept)
                acc[part, member, :, lanes] = kept

    def heads_at(step):
        local = step < 2 * block_steps
        chunk = step - 2 * block_steps
        base = block_groups * jnp.where(step < block_steps, s, twin) + STEP_GROUPS * (step % block_steps)
        heads = []
        for which in range(STEP_GROUPS):
            home = across if which < 2 else far
            side = x if which % 2 == 0 else other_x
            heads.append(jnp.where(local, base + which, block_groups * home + chunks * side + chunk))
        return heads

    last = 2 * block_steps + chunks - 1
    slow_until = 2 * block_steps + 6

    def pass_on(step):
        slow = step <= slow_until
        y_chunk = jnp.where(slow, (step - 4) // 2, step - slow_until + 9)
        x_chunk = jnp.where(slow, (step - 8) // 2, step - slow_until + 7)
        turn = jnp.logical_or(jnp.logical_not(slow), step % 2 == 0)

        @pl.when(turn & (step >= 4) & (y_chunk < chunks))
        def _():
            y_copy(y_chunk).wait_recv()
            x_copy(y_chunk).start()
            dy_copy(y_chunk).start()

        @pl.when(turn & (step >= 8) & (x_chunk < chunks))
        def _():
            x_copy(x_chunk).wait_recv()
            dx_copy(x_chunk).start()

        @pl.when((step >= block_steps) & (step < 2 * block_steps))
        def _():
            own_copy(step - block_steps).wait_recv()

        @pl.when(step >= 2 * block_steps)
        def _():
            dy_copy(step - 2 * block_steps).wait_recv()
            dx_copy(step - 2 * block_steps).wait_recv()

    def main(step, carry):
        pass_on(step)
        heads = heads_at(step)
        for part in range(dims):
            score(step, heads, part)
        return carry

    lax.fori_loop(0, last, main, 0)
    pass_on(last)
    last_heads = heads_at(jnp.int32(last))

    def finish(turn, carry):
        score(last, last_heads, target_at(turn))

        @pl.when(turn > 0)
        def _():
            part_copy(target_at(turn - 1), turn - 1).start()
        return carry

    lax.fori_loop(0, dims, finish, 0)

    for which in range(dims - 1):
        remote(acc.at[z], parts.at[which], send_r.at[which], recv_r.at[which], at()).wait_recv()

    scores, names = [], []
    for member in range(LIST_LEN):
        total = acc[z, member]
        for which in range(dims - 1):
            total = total + parts[which, member]
        name = cand_ids[member]
        real = name >= 0.0
        scores.append(jnp.where(real, total, -jnp.inf))
        names.append(jnp.where(real, name, BIG))
    for place in range(TOP_K):
        best = functools.reduce(jnp.maximum, scores)
        best = jnp.max(best, axis=0, keepdims=True)
        tied = [jnp.where(score_j == best, name_j, BIG) for score_j, name_j in zip(scores, names)]
        first = jnp.min(functools.reduce(jnp.minimum, tied), axis=0, keepdims=True)
        res[z, place:place + 1, :] = best
        res[z, TOP_K + place:TOP_K + place + 1, :] = first
        if place + 1 < TOP_K:
            scores = [jnp.where(name_j == first, -jnp.inf, score_j) for score_j, name_j in zip(scores, names)]

    def drain_local(block, carry):
        own_copy(block).wait_send()
        return carry

    def drain_chunks(chunk, carry):
        y_copy(chunk).wait_send()
        x_copy(chunk).wait_send()
        dy_copy(chunk).wait_send()
        dx_copy(chunk).wait_send()
        return carry

    lax.fori_loop(0, block_steps, drain_local, 0)
    lax.fori_loop(0, chunks, drain_chunks, 0)
    for which, peer in enumerate((twin, across, far)):
        id_copy(which, peer).wait_send()
    for which in range(dims - 1):
        part_copy(target_at(which), which).wait_send()

    for which in range(dims - 1):
        res_copy(target_at(which), which).start()
    for which in range(dims - 1):
        remote(res.at[z], res.at[(z + 1 + which) % dims], send_g.at[which], recv_g.at[which], at()).wait_recv()
    for part in range(dims):
        out_s[:, part * width:(part + 1) * width] = res[part, 0:TOP_K, :]
        out_i[:, part * width:(part + 1) * width] = res[part, TOP_K:2 * TOP_K, :].astype(jnp.int32)
    for which in range(dims - 1):
        res_copy(target_at(which), which).wait_send()


def solution(mesh):
    dims = mesh.shape['dim']
    row_spec = P(('rep', 'shard'), None)

    def local_search(queries, list_vecs, list_ids, probes):
        rows_q, depth = queries.shape
        lists_dev, list_len, _ = list_vecs.shape
        probe_count = probes.shape[1]
        block_rows = lists_dev * list_len
        block_steps = block_rows // STEP_ROWS
        chunks = lists_dev // GROUP_LISTS // 2
        width = rows_q // dims
        dma = pltpu.SemaphoreType.DMA
        any_spec = pl.BlockSpec(memory_space=pl.ANY)
        vmem_spec = pl.BlockSpec(memory_space=pltpu.VMEM)
        scores, ids = pl.pallas_call(
            functools.partial(search_kernel, dims),
            out_shape=(jax.ShapeDtypeStruct((TOP_K, rows_q), jnp.float32),
                       jax.ShapeDtypeStruct((TOP_K, rows_q), jnp.int32)),
            in_specs=[any_spec, any_spec, vmem_spec, vmem_spec],
            out_specs=(vmem_spec, vmem_spec),
            scratch_shapes=[
                pltpu.VMEM((block_rows, depth), jnp.bfloat16),
                pltpu.VMEM((rows_q, depth), jnp.bfloat16),
                pltpu.VMEM((4 * block_rows, depth), jnp.bfloat16),
                pltpu.VMEM((STEP_ROWS, STEP_ROWS), jnp.bfloat16),
                pltpu.VMEM((dims, LIST_LEN, probe_count, width), jnp.float32),
                pltpu.VMEM((dims - 1, LIST_LEN, probe_count, width), jnp.float32),
                pltpu.VMEM((4, LIST_LEN, lists_dev), jnp.int32),
                pltpu.VMEM((LIST_LEN, probe_count, width), jnp.float32),
                pltpu.VMEM((dims, 24, width), jnp.float32),
                dma((block_steps,)), dma((dims,)),
                dma((block_steps,)), dma((block_steps,)),
                dma((chunks,)), dma((chunks,)), dma((chunks,)), dma((chunks,)),
                dma((chunks,)), dma((chunks,)), dma((chunks,)), dma((chunks,)),
                dma((3,)), dma((3,)),
                dma((dims - 1,)), dma((dims - 1,)), dma((dims - 1,)), dma((dims - 1,)),
            ],
            compiler_params=pltpu.CompilerParams(collective_id=0, has_side_effects=True, vmem_limit_bytes=60 * 2**20),
            name='ivf_search',
        )(queries, list_vecs.reshape(block_rows, depth), probes.T, list_ids.T)
        return scores.T, ids.T

    return jax.shard_map(local_search, mesh=mesh,
                         in_specs=(P(('rep', 'shard'), 'dim'), P('shard', None, 'dim'), P('shard', None), row_spec),
                         out_specs=(row_spec, row_spec), check_vma=False)
```

time: 2550 us -> 88.3 us (0.03)
  local copies, waits for them, and re-layouts: 1070 us -> 3.14 us
  waiting for transfers between devices: 741 us -> 0 us
  matrix products: 661 us -> 0 us
  Pallas kernels: 0 us -> 84.3 us
    gather x22 -> x0, local copies, waits for them, and re-layouts: 917 us -> none  [the longest x16 424 us: per_block(): members = list_vecs[jnp.maximum(block_lists, 0)]]
    all_to_all x2 -> x0, waiting for transfers between devices: 721 us -> none  [the longest x1 721 us: local_search(): recv_rows = lax.all_to_all(send_rows, 'shard', 0, 0)]
    dot_general x16 -> x0, matrix products: 661 us -> none  [per_block(): jnp.einsum('cd,cjd->cj', block_rows, members, preferred_element_type=jnp....]
    pallas_call x0 -> x1, Pallas kernels: none -> 84.3 us  [local_search(): pl.pallas_call(functools.partial(search_kernel, dims), out_shape=(jax.Sha...]
    scatter x1 -> x0, local copies, waits for them, and re-layouts: 60.4 us -> none  [route_slots(): jnp.full((group_devs * slot_cap,), -1, jnp.int32).at[flat_slot]]
    squeeze x16 -> x0, local copies, waits for them, and re-layouts: 42 us -> none  [score_received(): block_scores = lax.map(per_block, (row_blocks, list_blocks))]
  transfers between devices with their start and end apart: 5 -> 0, of which waited for: 2 -> 0; matrix products, arithmetic and copies ran while one was open for 11% -> 0% of each run, Pallas kernels for 0% -> 0%
where the time goes in v1:
time: 88.3 us; the launch traced here: 88.1 us
  Pallas kernels  84.3 us (95%)
  local copies, waits for them, and re-layouts  3.14 us (4%)
    pallas_call x1, Pallas kernels, local_search(): pl.pallas_call(functools.partial(search_kernel, dims), out_shape=(jax.Sha...  84.3 us
    unnamed x2, local copies, waits for them, and re-layouts  3.14 us

profile of v1, /device:TPU:0, one launch (start us, length us, event | category | flops | bytes accessed | tf_op | source)
XLA Modules:
  0.0 88.1 jit_solution(1089653709971559779)
XLA Ops:
  0.6 84.3 %ivf_search.1 = (f32[10,2048]{1,0:T(8,128)}, s32[10,2048]{1,0:T(8,128)}) custom-call(bf16[2048,1024]{1,0:T(8,128)(2,1)} %q_hbm.1, bf16[2048,1024]{1,0:T(8,128)(2,1)} %bitcast.5, s32[8,2048]{1,0:T(8,128)} %bitcast.8, s32[8,256]{1,0:T(8,128)} %bitcast.9), custom_call_target="tpu_custom_call" | custom-call | tf_op jit(solution)/shard_map/ivf_search/pallas_call | solution.py:317
  84.9 1.6 %copy.8 = f32[2048,10]{0,1:T(8,128)} copy(f32[2048,10]{0,1:T(8,128)} %bitcast.7) | data formatting | bytes 163840
  86.5 1.6 %copy.9 = s32[2048,10]{0,1:T(8,128)} copy(s32[2048,10]{0,1:T(8,128)} %bitcast.6) | data formatting | bytes 163840

commit v2 on v1

--- a/solution.py
+++ b/solution.py
@@ -13,6 +13,7 @@
 GROUP_ROWS = GROUP_LISTS * LIST_LEN
 STEP_GROUPS = 4
 STEP_ROWS = STEP_GROUPS * GROUP_ROWS
+PIECE_ROWS = GROUP_ROWS // 2
 LANES = 128
 MESH = pl.DeviceIdType.MESH
 BIG = 1e9
@@ -22,8 +23,8 @@
     return index + bit - 2 * bit * ((index // bit) % 2)
 
 
-def search_kernel(dims, q_hbm, l_hbm, probes_ref, ids_ref, out_s, out_i,
-                  raw, qv, vecs, perm, acc, parts, ids_all, cand_ids, res,
+def search_kernel(dims, q_hbm, l_hbm, probes_ref, ids_ref, res,
+                  raw, qv, vecs, perm, acc, parts, ids_all, cand_ids,
                   load_l, load_q, send_o, recv_o, send_y, recv_y, send_x, recv_x,
                   send_dy, recv_dy, send_dx, recv_dx, send_i, recv_i,
                   send_r, recv_r, send_g, recv_g):
@@ -31,7 +32,7 @@
     lists_dev = ids_ref.shape[1]
     block_rows = lists_dev * LIST_LEN
     block_groups = lists_dev // GROUP_LISTS
-    chunks = block_groups // 2
+    chunks = block_groups
     block_steps = block_groups // STEP_GROUPS
     width = rows_q // dims
     x, z, s = lax.axis_index('rep'), lax.axis_index('dim'), lax.axis_index('shard')
@@ -41,9 +42,6 @@
     def at(**place):
         return {'rep': x, 'dim': z, 'shard': s, **place}
 
-    def group_rows(group):
-        return pl.ds(pl.multiple_of(group * GROUP_ROWS, GROUP_ROWS), GROUP_ROWS)
-
     def step_rows(step):
         return pl.ds(pl.multiple_of(step * STEP_ROWS, STEP_ROWS), STEP_ROWS)
 
@@ -62,11 +60,15 @@
         return remote(vecs.at[step_rows(block)], vecs.at[step_rows(block_steps + block)],
                       send_o.at[block], recv_o.at[block], at(shard=twin))
 
+    def piece(group, chunk):
+        first = pl.multiple_of(group * GROUP_ROWS + chunk % 2 * PIECE_ROWS, PIECE_ROWS)
+        return vecs.at[pl.ds(first, PIECE_ROWS)]
+
     def slot(chunk, which):
-        return vecs.at[group_rows(2 * block_groups + STEP_GROUPS * chunk + which)]
+        return piece(2 * block_groups + STEP_GROUPS * (chunk // 2) + which, chunk)
 
     def y_copy(chunk):
-        return remote(vecs.at[group_rows(chunks * x + chunk)], slot(chunk, 0), send_y.at[chunk], recv_y.at[chunk], at(shard=across))
+        return remote(piece(chunks // 2 * x + chunk // 2, chunk), slot(chunk, 0), send_y.at[chunk], recv_y.at[chunk], at(shard=across))
 
     def x_copy(chunk):
         return remote(slot(chunk, 0), slot(chunk, 1), send_x.at[chunk], recv_x.at[chunk], at(rep=other_x))
@@ -106,8 +108,6 @@
 
     for turn in range(block_steps):
         load_list(block_at(turn)).start()
-    for part in range(dims):
-        load_query(part).start()
 
     barrier = pltpu.get_barrier_semaphore()
     peers = [at(shard=twin), at(shard=across), at(shard=far), at(rep=other_x)]
@@ -119,33 +119,36 @@
     col = lax.broadcasted_iota(jnp.int32, (STEP_ROWS, STEP_ROWS), 1)
     source = (row // GROUP_ROWS) * GROUP_ROWS + (row % GROUP_LISTS) * LIST_LEN + (row // GROUP_LISTS) % LIST_LEN
     perm[...] = jnp.where(col == source, 1.0, 0.0).astype(jnp.bfloat16)
-    acc[...] = jnp.zeros_like(acc)
-    ids_all[s] = ids_ref[...]
-
-    pl.semaphore_wait(barrier, len(peers))
-    for which, peer in enumerate((twin, across, far)):
-        id_copy(which, peer).start()
 
     def send_block(turn):
+        @pl.when(turn < block_steps // 2)
+        def _():
+            for sub in range(2 * STEP_GROUPS):
+                y_copy(2 * STEP_GROUPS * turn + sub).start()
         own_copy(block_at(turn)).start()
 
-        @pl.when(turn < block_steps // 2)
-        def _():
-            for sub in range(STEP_GROUPS):
-                y_copy(STEP_GROUPS * turn + sub).start()
-
-    def arrange(turn, carry):
+    def arrange(turn):
         block = block_at(turn)
         load_list(block).wait()
         moved = jnp.dot(perm[...], raw[step_rows(block), :], preferred_element_type=jnp.float32)
         vecs[step_rows(block), :] = moved.astype(jnp.bfloat16)
 
-        @pl.when(turn > 0)
-        def _():
-            send_block(turn - 1)
-        return carry
-
-    lax.fori_loop(0, block_steps, arrange, 0)
+    arrange(0)
+    for part in range(dims):
+        load_query(part).start()
+    ids_all[s] = ids_ref[...]
+    pl.semaphore_wait(barrier, len(peers))
+
+    def arrange_send(turn, carry):
+        arrange(turn)
+        send_block(turn - 1)
+        return carry
+
+    lax.fori_loop(1, block_steps, arrange_send, 0)
+    for which, peer in enumerate((twin, across, far)):
+        id_copy(which, peer).start()
+    acc[...] = jnp.zeros_like(acc)
+    send_block(block_steps - 1)
 
     for part in range(dims):
         load_query(part).wait()
@@ -168,7 +171,6 @@
         return carry
 
     lax.fori_loop(0, width // LANES, name_candidates, 0)
-    send_block(block_steps - 1)
 
     def score(step, heads, part):
         lists = vecs[step_rows(step), :]
@@ -189,34 +191,47 @@
 
     def heads_at(step):
         local = step < 2 * block_steps
-        chunk = step - 2 * block_steps
+        group = step - 2 * block_steps
         base = block_groups * jnp.where(step < block_steps, s, twin) + STEP_GROUPS * (step % block_steps)
         heads = []
         for which in range(STEP_GROUPS):
             home = across if which < 2 else far
             side = x if which % 2 == 0 else other_x
-            heads.append(jnp.where(local, base + which, block_groups * home + chunks * side + chunk))
+            heads.append(jnp.where(local, base + which, block_groups * home + chunks // 2 * side + group))
         return heads
 
-    last = 2 * block_steps + chunks - 1
-    slow_until = 2 * block_steps + 6
+    last = 2 * block_steps + chunks // 2 - 1
+    paced = last - 4
+
+    def pass_y(chunk):
+        y_copy(chunk).wait_recv()
+        x_copy(chunk).start()
+        dy_copy(chunk).start()
+
+    def pass_x(chunk):
+        x_copy(chunk).wait_recv()
+        dx_copy(chunk).start()
 
     def pass_on(step):
-        slow = step <= slow_until
-        y_chunk = jnp.where(slow, (step - 4) // 2, step - slow_until + 9)
-        x_chunk = jnp.where(slow, (step - 8) // 2, step - slow_until + 7)
-        turn = jnp.logical_or(jnp.logical_not(slow), step % 2 == 0)
-
-        @pl.when(turn & (step >= 4) & (y_chunk < chunks))
-        def _():
-            y_copy(y_chunk).wait_recv()
-            x_copy(y_chunk).start()
-            dy_copy(y_chunk).start()
-
-        @pl.when(turn & (step >= 8) & (x_chunk < chunks))
-        def _():
-            x_copy(x_chunk).wait_recv()
-            dx_copy(x_chunk).start()
+        @pl.when((step >= 1) & (step < paced))
+        def _():
+            pass_y(step - 1)
+
+        @pl.when((step >= 4) & (step <= paced))
+        def _():
+            pass_x(step - 4)
+
+        @pl.when((step >= paced) & (step < paced + 3))
+        def _():
+            first = chunks - 6 + 2 * (step - paced)
+            pass_y(first)
+            pass_x(first - 2)
+            pass_y(first + 1)
+            pass_x(first - 1)
+
+        @pl.when(step >= paced + 3)
+        def _():
+            pass_x(step - last + chunks - 1)
 
         @pl.when((step >= block_steps) & (step < 2 * block_steps))
         def _():
@@ -224,8 +239,10 @@
 
         @pl.when(step >= 2 * block_steps)
         def _():
-            dy_copy(step - 2 * block_steps).wait_recv()
-            dx_copy(step - 2 * block_steps).wait_recv()
+            first = 2 * (step - 2 * block_steps)
+            for chunk in (first, first + 1):
+                dy_copy(chunk).wait_recv()
+                dx_copy(chunk).wait_recv()
 
     def main(step, carry):
         pass_on(step)
@@ -292,11 +309,16 @@
         res_copy(target_at(which), which).start()
     for which in range(dims - 1):
         remote(res.at[z], res.at[(z + 1 + which) % dims], send_g.at[which], recv_g.at[which], at()).wait_recv()
+    for which in range(dims - 1):
+        res_copy(target_at(which), which).wait_send()
+
+
+def place_kernel(res, out_s, out_i):
+    dims, _, width = res.shape
     for part in range(dims):
-        out_s[:, part * width:(part + 1) * width] = res[part, 0:TOP_K, :]
-        out_i[:, part * width:(part + 1) * width] = res[part, TOP_K:2 * TOP_K, :].astype(jnp.int32)
-    for which in range(dims - 1):
-        res_copy(target_at(which), which).wait_send()
+        cols = slice(part * width, (part + 1) * width)
+        out_s[:, cols] = res[part, 0:TOP_K, :]
+        out_i[:, cols] = res[part, TOP_K:2 * TOP_K, :].astype(jnp.int32)
 
 
 def solution(mesh):
@@ -309,17 +331,16 @@
         probe_count = probes.shape[1]
         block_rows = lists_dev * list_len
         block_steps = block_rows // STEP_ROWS
-        chunks = lists_dev // GROUP_LISTS // 2
+        chunks = lists_dev // GROUP_LISTS
         width = rows_q // dims
         dma = pltpu.SemaphoreType.DMA
         any_spec = pl.BlockSpec(memory_space=pl.ANY)
         vmem_spec = pl.BlockSpec(memory_space=pltpu.VMEM)
-        scores, ids = pl.pallas_call(
+        found = pl.pallas_call(
             functools.partial(search_kernel, dims),
-            out_shape=(jax.ShapeDtypeStruct((TOP_K, rows_q), jnp.float32),
-                       jax.ShapeDtypeStruct((TOP_K, rows_q), jnp.int32)),
+            out_shape=jax.ShapeDtypeStruct((dims, 2 * TOP_K, width), jnp.float32),
             in_specs=[any_spec, any_spec, vmem_spec, vmem_spec],
-            out_specs=(vmem_spec, vmem_spec),
+            out_specs=vmem_spec,
             scratch_shapes=[
                 pltpu.VMEM((block_rows, depth), jnp.bfloat16),
                 pltpu.VMEM((rows_q, depth), jnp.bfloat16),
@@ -329,7 +350,6 @@
                 pltpu.VMEM((dims - 1, LIST_LEN, probe_count, width), jnp.float32),
                 pltpu.VMEM((4, LIST_LEN, lists_dev), jnp.int32),
                 pltpu.VMEM((LIST_LEN, probe_count, width), jnp.float32),
-                pltpu.VMEM((dims, 24, width), jnp.float32),
                 dma((block_steps,)), dma((dims,)),
                 dma((block_steps,)), dma((block_steps,)),
                 dma((chunks,)), dma((chunks,)), dma((chunks,)), dma((chunks,)),
@@ -340,6 +360,14 @@
             compiler_params=pltpu.CompilerParams(collective_id=0, has_side_effects=True, vmem_limit_bytes=60 * 2**20),
             name='ivf_search',
         )(queries, list_vecs.reshape(block_rows, depth), probes.T, list_ids.T)
+        scores, ids = pl.pallas_call(
+            place_kernel,
+            out_shape=(jax.ShapeDtypeStruct((TOP_K, rows_q), jnp.float32),
+                       jax.ShapeDtypeStruct((TOP_K, rows_q), jnp.int32)),
+            in_specs=[vmem_spec],
+            out_specs=(vmem_spec, vmem_spec),
+            name='place',
+        )(found)
         return scores.T, ids.T
 
     return jax.shard_map(local_search, mesh=mesh,

time: 88.3 us -> 129 us (1.46)
  Pallas kernels: 84.3 us -> 128 us
  local copies, waits for them, and re-layouts: 3.14 us -> 0 us
    pallas_call x1 -> x2, Pallas kernels: 84.3 us -> 128 us  [the longest x1 126 us: local_search(): pl.pallas_call(functools.partial(search_kernel, dims), out_shape=jax.Shap...]
    unnamed x2 -> x0, local copies, waits for them, and re-layouts: 3.14 us -> none
where the time goes in v2:
time: 129 us; the launch traced here: 128 us
  Pallas kernels  128 us (99%)
    pallas_call x1, Pallas kernels, local_search(): pl.pallas_call(functools.partial(search_kernel, dims), out_shape=jax.Shap...  126 us

profile of v2, /device:TPU:0, one launch (start us, length us, event | category | flops | bytes accessed | tf_op | source)
XLA Modules:
  0.0 128.5 jit_solution(2337497535327225886)
XLA Ops:
  0.6 126.2 %ivf_search.1.res = f32[4,20,512]{2,1,0:T(8,128)} custom-call(bf16[2048,1024]{1,0:T(8,128)(2,1)} %q_hbm.1, bf16[2048,1024]{1,0:T(8,128)(2,1)} %bitcast.5, s32[8,2048]{1,0:T(8,128)} %bitcast.6, s32[8,256]{1,0:T(8,128)} %bitcast.7), custom_call_target="tpu_custom_call" | custom-call | tf_op jit(solution)/shard_map/ivf_search/pallas_call | solution.py:339
  126.8 1.6 %place.1 = (f32[10,2048]{1,0:T(8,128)}, s32[10,2048]{1,0:T(8,128)}) custom-call(f32[4,20,512]{2,1,0:T(8,128)} %ivf_search.1.res), custom_call_target="tpu_custom_call" | custom-call | tf_op jit(solution)/shard_map/place/pallas_call | solution.py:363

commit v3 on v2

--- a/solution.py
+++ b/solution.py
@@ -120,11 +120,13 @@
     source = (row // GROUP_ROWS) * GROUP_ROWS + (row % GROUP_LISTS) * LIST_LEN + (row // GROUP_LISTS) % LIST_LEN
     perm[...] = jnp.where(col == source, 1.0, 0.0).astype(jnp.bfloat16)
 
+    window = 2 * STEP_GROUPS
+
     def send_block(turn):
-        @pl.when(turn < block_steps // 2)
-        def _():
-            for sub in range(2 * STEP_GROUPS):
-                y_copy(2 * STEP_GROUPS * turn + sub).start()
+        @pl.when(turn == 0)
+        def _():
+            for chunk in range(window):
+                y_copy(chunk).start()
         own_copy(block_at(turn)).start()
 
     def arrange(turn):
@@ -207,6 +209,10 @@
         y_copy(chunk).wait_recv()
         x_copy(chunk).start()
         dy_copy(chunk).start()
+
+        @pl.when(chunk + window < chunks)
+        def _():
+            y_copy(chunk + window).start()
 
     def pass_x(chunk):
         x_copy(chunk).wait_recv()

time: 129 us -> 95 us (0.74)
  Pallas kernels: 128 us -> 94.2 us
    pallas_call x1, Pallas kernels: 126 us -> 92.5 us  [local_search(): pl.pallas_call(functools.partial(search_kernel, dims), out_shape=jax.Shap...]
where the time goes in v3:
time: 95 us; the launch traced here: 94.8 us
  Pallas kernels  94.2 us (99%)
    pallas_call x1, Pallas kernels, local_search(): pl.pallas_call(functools.partial(search_kernel, dims), out_shape=jax.Shap...  92.5 us

profile of v3, /device:TPU:0, one launch (start us, length us, event | category | flops | bytes accessed | tf_op | source)
XLA Modules:
  0.0 94.8 jit_solution(15680485064499359141)
XLA Ops:
  0.6 92.5 %ivf_search.1.res = f32[4,20,512]{2,1,0:T(8,128)} custom-call(bf16[2048,1024]{1,0:T(8,128)(2,1)} %q_hbm.1, bf16[2048,1024]{1,0:T(8,128)(2,1)} %bitcast.5, s32[8,2048]{1,0:T(8,128)} %bitcast.6, s32[8,256]{1,0:T(8,128)} %bitcast.7), custom_call_target="tpu_custom_call" | custom-call | tf_op jit(solution)/shard_map/ivf_search/pallas_call | solution.py:345
  93.2 1.6 %place.1 = (f32[10,2048]{1,0:T(8,128)}, s32[10,2048]{1,0:T(8,128)}) custom-call(f32[4,20,512]{2,1,0:T(8,128)} %ivf_search.1.res), custom_call_target="tpu_custom_call" | custom-call | tf_op jit(solution)/shard_map/place/pallas_call | solution.py:369

commit v4 on v3

--- a/solution.py
+++ b/solution.py
@@ -106,7 +106,10 @@
     def block_at(turn):
         return (block_steps // 2 * x + turn) % block_steps
 
-    for turn in range(block_steps):
+    load_list(block_at(0)).start()
+    for part in range(dims):
+        load_query(part).start()
+    for turn in range(1, block_steps):
         load_list(block_at(turn)).start()
 
     barrier = pltpu.get_barrier_semaphore()
@@ -120,42 +123,23 @@
     source = (row // GROUP_ROWS) * GROUP_ROWS + (row % GROUP_LISTS) * LIST_LEN + (row // GROUP_LISTS) % LIST_LEN
     perm[...] = jnp.where(col == source, 1.0, 0.0).astype(jnp.bfloat16)
 
-    window = 2 * STEP_GROUPS
-
-    def send_block(turn):
-        @pl.when(turn == 0)
-        def _():
-            for chunk in range(window):
-                y_copy(chunk).start()
-        own_copy(block_at(turn)).start()
-
     def arrange(turn):
         block = block_at(turn)
-        load_list(block).wait()
         moved = jnp.dot(perm[...], raw[step_rows(block), :], preferred_element_type=jnp.float32)
         vecs[step_rows(block), :] = moved.astype(jnp.bfloat16)
 
+    window = 2 * STEP_GROUPS
+    load_list(block_at(0)).wait()
     arrange(0)
-    for part in range(dims):
-        load_query(part).start()
+    pl.semaphore_wait(barrier, len(peers))
+    for chunk in range(window):
+        y_copy(chunk).start()
     ids_all[s] = ids_ref[...]
-    pl.semaphore_wait(barrier, len(peers))
-
-    def arrange_send(turn, carry):
-        arrange(turn)
-        send_block(turn - 1)
-        return carry
-
-    lax.fori_loop(1, block_steps, arrange_send, 0)
+    acc[...] = jnp.zeros_like(acc)
     for which, peer in enumerate((twin, across, far)):
         id_copy(which, peer).start()
-    acc[...] = jnp.zeros_like(acc)
-    send_block(block_steps - 1)
-
     for part in range(dims):
         load_query(part).wait()
-    for which, peer in enumerate((twin, across, far)):
-        remote(ids_ref, ids_all.at[peer], send_i.at[which], recv_i.at[which], at(shard=peer)).wait_recv()
 
     def name_candidates(tile, carry):
         cols = pl.ds(pl.multiple_of(z * width + tile * LANES, LANES), LANES)
@@ -172,10 +156,11 @@
             cand_ids[member, :, pl.ds(pl.multiple_of(tile * LANES, LANES), LANES)] = got.astype(jnp.float32)
         return carry
 
-    lax.fori_loop(0, width // LANES, name_candidates, 0)
+    def list_block(step):
+        return jnp.where(step < block_steps, block_at(step), step % block_steps)
 
     def score(step, heads, part):
-        lists = vecs[step_rows(step), :]
+        lists = vecs[step_rows(jnp.where(step < block_steps, block_at(step), step)), :]
         rows = pl.ds(pl.multiple_of(part * width, width), width)
         scores = lax.dot_general(lists, qv[rows, :], (((1,), (1,)), ((), ())), preferred_element_type=jnp.float32)
         for tile in range(width // LANES):
@@ -194,7 +179,7 @@
     def heads_at(step):
         local = step < 2 * block_steps
         group = step - 2 * block_steps
-        base = block_groups * jnp.where(step < block_steps, s, twin) + STEP_GROUPS * (step % block_steps)
+        base = block_groups * jnp.where(step < block_steps, s, twin) + STEP_GROUPS * list_block(step)
         heads = []
         for which in range(STEP_GROUPS):
             home = across if which < 2 else far
@@ -203,7 +188,6 @@
         return heads
 
     last = 2 * block_steps + chunks // 2 - 1
-    paced = last - 4
 
     def pass_y(chunk):
         y_copy(chunk).wait_recv()
@@ -218,55 +202,90 @@
         x_copy(chunk).wait_recv()
         dx_copy(chunk).start()
 
-    def pass_on(step):
-        @pl.when((step >= 1) & (step < paced))
-        def _():
-            pass_y(step - 1)
-
-        @pl.when((step >= 4) & (step <= paced))
-        def _():
-            pass_x(step - 4)
-
-        @pl.when((step >= paced) & (step < paced + 3))
-        def _():
-            first = chunks - 6 + 2 * (step - paced)
-            pass_y(first)
-            pass_x(first - 2)
-            pass_y(first + 1)
-            pass_x(first - 1)
-
-        @pl.when(step >= paced + 3)
-        def _():
-            pass_x(step - last + chunks - 1)
-
-        @pl.when((step >= block_steps) & (step < 2 * block_steps))
-        def _():
-            own_copy(step - block_steps).wait_recv()
-
-        @pl.when(step >= 2 * block_steps)
-        def _():
-            first = 2 * (step - 2 * block_steps)
-            for chunk in (first, first + 1):
-                dy_copy(chunk).wait_recv()
-                dx_copy(chunk).wait_recv()
-
-    def main(step, carry):
-        pass_on(step)
+    def await_step(step):
+        first = 2 * (step - 2 * block_steps)
+        for chunk in (first, first + 1):
+            dy_copy(chunk).wait_recv()
+            dx_copy(chunk).wait_recv()
+
+    def score_all(step):
         heads = heads_at(step)
         for part in range(dims):
             score(step, heads, part)
-        return carry
-
-    lax.fori_loop(0, last, main, 0)
-    pass_on(last)
+
+    def early(step, carry):
+        own_copy(block_at(step)).start()
+
+        @pl.when(step >= 2)
+        def _():
+            pass_y(jnp.where(step <= 5, step - 2, step - 1))
+
+        @pl.when(step == 5)
+        def _():
+            pass_y(4)
+
+        @pl.when(step >= 5)
+        def _():
+            pass_x(step - 5)
+        load_list(block_at(step + 1)).wait()
+        score_all(step)
+        arrange(step + 1)
+        return carry
+
+    def middle(step, carry):
+        pass_y(step - 1)
+        pass_x(step - 5)
+
+        @pl.when(step == block_steps - 1)
+        def _():
+            own_copy(block_at(step)).start()
+
+        @pl.when((step >= block_steps) & (step < 2 * block_steps))
+        def _():
+            own_copy(step - block_steps).wait_recv()
+
+        @pl.when(step >= 2 * block_steps)
+        def _():
+            await_step(step)
+        score_all(step)
+        return carry
+
+    late_plan = {
+        last - 5: 'y25 x21 x22',
+        last - 4: 'y26 y27 x23',
+        last - 3: 'y28 y29 x24 x25 y30',
+        last - 2: 'y31 x26 x27',
+        last - 1: 'x28 x29 x30',
+    }
+
+    def late(step, carry):
+        for when, plan in late_plan.items():
+            @pl.when(step == when)
+            def _(plan=plan):
+                for word in plan.split():
+                    (pass_y if word[0] == 'y' else pass_x)(int(word[1:]))
+
+        @pl.when(step == last - 1)
+        def _():
+            for which, peer in enumerate((twin, across, far)):
+                remote(ids_ref, ids_all.at[peer], send_i.at[which], recv_i.at[which], at(shard=peer)).wait_recv()
+            lax.fori_loop(0, width // LANES, name_candidates, 0)
+        await_step(step)
+        score_all(step)
+        return carry
+
+    lax.fori_loop(0, block_steps - 1, early, 0)
+    lax.fori_loop(block_steps - 1, last - 5, middle, 0)
+    lax.fori_loop(last - 5, last, late, 0)
+    pass_x(chunks - 1)
+    await_step(jnp.int32(last))
     last_heads = heads_at(jnp.int32(last))
 
     def finish(turn, carry):
-        score(last, last_heads, target_at(turn))
-
         @pl.when(turn > 0)
         def _():
             part_copy(target_at(turn - 1), turn - 1).start()
+        score(jnp.int32(last), last_heads, target_at(turn))
         return carry
 
     lax.fori_loop(0, dims, finish, 0)

time: 95 us -> 85.2 us (0.90)
  Pallas kernels: 94.2 us -> 84.4 us
    pallas_call x1, Pallas kernels: 92.5 us -> 82.8 us  [local_search(): pl.pallas_call(functools.partial(search_kernel, dims), out_shape=jax.Shap...]
where the time goes in v4:
time: 85.2 us; the launch traced here: 85 us
  Pallas kernels  84.4 us (99%)
    pallas_call x1, Pallas kernels, local_search(): pl.pallas_call(functools.partial(search_kernel, dims), out_shape=jax.Shap...  82.8 us

profile of v4, /device:TPU:0, one launch (start us, length us, event | category | flops | bytes accessed | tf_op | source)
XLA Modules:
  0.0 85.0 jit_solution(13898437937051102495)
XLA Ops:
  0.6 82.8 %ivf_search.1.res = f32[4,20,512]{2,1,0:T(8,128)} custom-call(bf16[2048,1024]{1,0:T(8,128)(2,1)} %q_hbm.1, bf16[2048,1024]{1,0:T(8,128)(2,1)} %bitcast.5, s32[8,2048]{1,0:T(8,128)} %bitcast.6, s32[8,256]{1,0:T(8,128)} %bitcast.7), custom_call_target="tpu_custom_call" | custom-call | tf_op jit(solution)/shard_map/ivf_search/pallas_call | solution.py:364
  83.4 1.6 %place.1 = (f32[10,2048]{1,0:T(8,128)}, s32[10,2048]{1,0:T(8,128)}) custom-call(f32[4,20,512]{2,1,0:T(8,128)} %ivf_search.1.res), custom_call_target="tpu_custom_call" | custom-call | tf_op jit(solution)/shard_map/place/pallas_call | solution.py:388

commit v5 on v4

--- a/solution.py
+++ b/solution.py
@@ -23,8 +23,8 @@
     return index + bit - 2 * bit * ((index // bit) % 2)
 
 
-def search_kernel(dims, q_hbm, l_hbm, probes_ref, ids_ref, res,
-                  raw, qv, vecs, perm, acc, parts, ids_all, cand_ids,
+def search_kernel(dims, q_hbm, l_hbm, probes_hbm, ids_hbm, res,
+                  raw, qv, vecs, perm, acc, parts, ids_all, cand_ids, probes_ref, ids_ref, load_p, load_i,
                   load_l, load_q, send_o, recv_o, send_y, recv_y, send_x, recv_x,
                   send_dy, recv_dy, send_dx, recv_dx, send_i, recv_i,
                   send_r, recv_r, send_g, recv_g):
@@ -82,31 +82,39 @@
     def id_copy(which, peer):
         return remote(ids_ref, ids_all.at[s], send_i.at[which], recv_i.at[which], at(shard=peer))
 
+    outer = z % 3 == 0
+    mate, far_outer = flip(z, 1), jnp.where(z < 2, dims - 1, 0)
+    far_inner = flip(far_outer, 1)
+    halves = tuple(pl.ds(half * (LIST_LEN // 2), LIST_LEN // 2) for half in range(2))
+
+    def part_copy(target, place, which, half):
+        return remote(acc.at[target, halves[half]], parts.at[place, halves[half]], send_r.at[which, half], recv_r.at[place, half], at(dim=mate))
+
+    def merged_copy(merge, half):
+        return remote(parts.at[merge, halves[half]], parts.at[3, halves[half]], send_r.at[1 + merge, half], recv_r.at[3, half],
+                      at(dim=(far_outer, far_inner)[merge]))
+
+    def part_wait(place, half):
+        remote(acc.at[z, halves[half]], parts.at[place, halves[half]], send_r.at[0, half], recv_r.at[place, half], at()).wait_recv()
+
     def peer_slot(source, target):
         return (source - target - 1 + dims) % dims
 
-    def part_copy(target, which):
-        return remote(acc.at[target], parts.at[peer_slot(z, target)], send_r.at[which], recv_r.at[peer_slot(z, target)], at(dim=target))
-
     def res_copy(target, which):
         return remote(res.at[z], res.at[z], send_g.at[which], recv_g.at[peer_slot(z, target)], at(dim=target))
 
     def target_at(turn):
-        if dims == 1:
-            return 0
-        half = dims // 2
-        low = z // half == 0
-        ahead = turn
-        far_target = jnp.where(low, dims - 1 - ahead, ahead)
-        near = turn - half
-        base = jnp.where(low, 0, half)
-        near_target = base + (z - base + 1 + near) % half
-        return jnp.where(turn < half, far_target, near_target)
+        first, second, third = (jnp.where(outer, one, two) for one, two in ((far_outer, mate), (far_inner, far_outer), (mate, far_inner)))
+        return jnp.where(turn == 0, first, jnp.where(turn == 1, second, jnp.where(turn == 2, third, z)))
 
     def block_at(turn):
         return (block_steps // 2 * x + turn) % block_steps
 
     load_list(block_at(0)).start()
+    probes_in = pltpu.make_async_copy(probes_hbm, probes_ref, load_p)
+    ids_in = pltpu.make_async_copy(ids_hbm, ids_ref, load_i)
+    ids_in.start()
+    probes_in.start()
     for part in range(dims):
         load_query(part).start()
     for turn in range(1, block_steps):
@@ -134,10 +142,12 @@
     pl.semaphore_wait(barrier, len(peers))
     for chunk in range(window):
         y_copy(chunk).start()
-    ids_all[s] = ids_ref[...]
     acc[...] = jnp.zeros_like(acc)
+    ids_in.wait()
     for which, peer in enumerate((twin, across, far)):
         id_copy(which, peer).start()
+    ids_all[s] = ids_ref[...]
+    probes_in.wait()
     for part in range(dims):
         load_query(part).wait()
 
@@ -282,22 +292,32 @@
     last_heads = heads_at(jnp.int32(last))
 
     def finish(turn, carry):
-        @pl.when(turn > 0)
-        def _():
-            part_copy(target_at(turn - 1), turn - 1).start()
+        @pl.when((turn > 0) & (outer | (turn == 1)))
+        def _():
+            for half in range(2):
+                part_copy(target_at(turn - 1), jnp.where(outer, turn - 1, 2), turn - 1, half).start()
         score(jnp.int32(last), last_heads, target_at(turn))
         return carry
 
     lax.fori_loop(0, dims, finish, 0)
 
-    for which in range(dims - 1):
-        remote(acc.at[z], parts.at[which], send_r.at[which], recv_r.at[which], at()).wait_recv()
-
+    @pl.when(jnp.logical_not(outer))
+    def _():
+        for merge, target in enumerate((far_outer, far_inner)):
+            for half in range(2):
+                part_wait(merge, half)
+                parts[merge, halves[half]] += acc[target, halves[half]]
+                merged_copy(merge, half).start()
+
+    for place in (2, 3):
+        for half in range(2):
+            part_wait(place, half)
+
+    tiles = width // LANES
     scores, names = [], []
     for member in range(LIST_LEN):
         total = acc[z, member]
-        for which in range(dims - 1):
-            total = total + parts[which, member]
+        total = total + parts[2, member] + parts[3, member]
         name = cand_ids[member]
         real = name >= 0.0
         scores.append(jnp.where(real, total, -jnp.inf))
@@ -307,8 +327,11 @@
         best = jnp.max(best, axis=0, keepdims=True)
         tied = [jnp.where(score_j == best, name_j, BIG) for score_j, name_j in zip(scores, names)]
         first = jnp.min(functools.reduce(jnp.minimum, tied), axis=0, keepdims=True)
-        res[z, place:place + 1, :] = best
-        res[z, TOP_K + place:TOP_K + place + 1, :] = first
+        for tile in range(tiles):
+            lanes = slice(tile * LANES, (tile + 1) * LANES)
+            line = place * tiles + tile
+            res[z, line:line + 1, :] = best[:, lanes]
+            res[z, TOP_K * tiles + line:TOP_K * tiles + line + 1, :] = first[:, lanes]
         if place + 1 < TOP_K:
             scores = [jnp.where(name_j == first, -jnp.inf, score_j) for score_j, name_j in zip(scores, names)]
 
@@ -327,8 +350,9 @@
     lax.fori_loop(0, chunks, drain_chunks, 0)
     for which, peer in enumerate((twin, across, far)):
         id_copy(which, peer).wait_send()
-    for which in range(dims - 1):
-        part_copy(target_at(which), which).wait_send()
+    for which in range(3):
+        for half in range(2):
+            part_copy(z, 2, which, half).wait_send()
 
     for which in range(dims - 1):
         res_copy(target_at(which), which).start()
@@ -339,11 +363,13 @@
 
 
 def place_kernel(res, out_s, out_i):
-    dims, _, width = res.shape
+    dims, lines, _ = res.shape
+    tiles = lines // (2 * TOP_K)
     for part in range(dims):
-        cols = slice(part * width, (part + 1) * width)
-        out_s[:, cols] = res[part, 0:TOP_K, :]
-        out_i[:, cols] = res[part, TOP_K:2 * TOP_K, :].astype(jnp.int32)
+        for tile in range(tiles):
+            first = (part * tiles + tile) * LANES
+            out_s[:, first:first + LANES] = res[part, pl.ds(tile, TOP_K, stride=tiles), :]
+            out_i[:, first:first + LANES] = res[part, pl.ds(TOP_K * tiles + tile, TOP_K, stride=tiles), :].astype(jnp.int32)
 
 
 def solution(mesh):
@@ -363,8 +389,8 @@
         vmem_spec = pl.BlockSpec(memory_space=pltpu.VMEM)
         found = pl.pallas_call(
             functools.partial(search_kernel, dims),
-            out_shape=jax.ShapeDtypeStruct((dims, 2 * TOP_K, width), jnp.float32),
-            in_specs=[any_spec, any_spec, vmem_spec, vmem_spec],
+            out_shape=pltpu.VMEM((dims, 2 * TOP_K * width // LANES, LANES), jnp.float32),
+            in_specs=[any_spec] * 4,
             out_specs=vmem_spec,
             scratch_shapes=[
                 pltpu.VMEM((block_rows, depth), jnp.bfloat16),
@@ -372,15 +398,18 @@
                 pltpu.VMEM((4 * block_rows, depth), jnp.bfloat16),
                 pltpu.VMEM((STEP_ROWS, STEP_ROWS), jnp.bfloat16),
                 pltpu.VMEM((dims, LIST_LEN, probe_count, width), jnp.float32),
-                pltpu.VMEM((dims - 1, LIST_LEN, probe_count, width), jnp.float32),
+                pltpu.VMEM((4, LIST_LEN, probe_count, width), jnp.float32),
                 pltpu.VMEM((4, LIST_LEN, lists_dev), jnp.int32),
                 pltpu.VMEM((LIST_LEN, probe_count, width), jnp.float32),
+                pltpu.VMEM((probe_count, rows_q), jnp.int32),
+                pltpu.VMEM((LIST_LEN, lists_dev), jnp.int32),
+                dma, dma,
                 dma((block_steps,)), dma((dims,)),
                 dma((block_steps,)), dma((block_steps,)),
                 dma((chunks,)), dma((chunks,)), dma((chunks,)), dma((chunks,)),
                 dma((chunks,)), dma((chunks,)), dma((chunks,)), dma((chunks,)),
                 dma((3,)), dma((3,)),
-                dma((dims - 1,)), dma((dims - 1,)), dma((dims - 1,)), dma((dims - 1,)),
+                dma((3, 2)), dma((4, 2)), dma((dims - 1,)), dma((dims - 1,)),
             ],
             compiler_params=pltpu.CompilerParams(collective_id=0, has_side_effects=True, vmem_limit_bytes=60 * 2**20),
             name='ivf_search',
@@ -391,6 +420,7 @@
                        jax.ShapeDtypeStruct((TOP_K, rows_q), jnp.int32)),
             in_specs=[vmem_spec],
             out_specs=(vmem_spec, vmem_spec),
+            compiler_params=pltpu.CompilerParams(vmem_limit_bytes=4 * 2**20),
             name='place',
         )(found)
         return scores.T, ids.T

time: 85.2 us -> 81 us (0.951)
  Pallas kernels: 84.4 us -> 80.2 us
    pallas_call x1, Pallas kernels: 82.8 us -> 79.5 us  [local_search(): pl.pallas_call(functools.partial(search_kernel, dims), out_shape=pltpu.VM...]
    pallas_call x1, Pallas kernels: 1.64 us -> 0.72 us  [local_search(): pl.pallas_call(place_kernel, out_shape=(jax.ShapeDtypeStruct((TOP_K, rows...]
where the time goes in v5:
time: 81 us; the launch traced here: 80.8 us
  Pallas kernels  80.2 us (99%)
    pallas_call x1, Pallas kernels, local_search(): pl.pallas_call(functools.partial(search_kernel, dims), out_shape=pltpu.VM...  79.5 us

profile of v5, /device:TPU:0, one launch (start us, length us, event | category | flops | bytes accessed | tf_op | source)
XLA Modules:
  0.0 80.8 jit_solution(11030668642240494915)
XLA Ops:
  0.6 79.5 %ivf_search.1.res = f32[4,80,128]{2,1,0:T(8,128)S(1)} custom-call(bf16[2048,1024]{1,0:T(8,128)(2,1)} %q_hbm.1, bf16[2048,1024]{1,0:T(8,128)(2,1)} %bitcast.5, s32[8,2048]{1,0:T(8,128)} %bitcast.6, s32[8,256]{1,0:T(8,128)} %bitcast.7), custom_call_target="tpu_custom_call" | custom-call | tf_op jit(solution)/shard_map/ivf_search/pallas_call | solution.py:390
  80.1 0.7 place.1

commit v6 on v5

--- a/solution.py
+++ b/solution.py
@@ -85,23 +85,22 @@
     outer = z % 3 == 0
     mate, far_outer = flip(z, 1), jnp.where(z < 2, dims - 1, 0)
     far_inner = flip(far_outer, 1)
-    halves = tuple(pl.ds(half * (LIST_LEN // 2), LIST_LEN // 2) for half in range(2))
 
     def part_copy(target, place, which, half):
-        return remote(acc.at[target, halves[half]], parts.at[place, halves[half]], send_r.at[which, half], recv_r.at[place, half], at(dim=mate))
+        return remote(acc.at[target, half], parts.at[place, half], send_r.at[which, half], recv_r.at[place, half], at(dim=mate))
 
     def merged_copy(merge, half):
-        return remote(parts.at[merge, halves[half]], parts.at[3, halves[half]], send_r.at[1 + merge, half], recv_r.at[3, half],
+        return remote(parts.at[merge, half], parts.at[3, half], send_r.at[1 + merge, half], recv_r.at[3, half],
                       at(dim=(far_outer, far_inner)[merge]))
 
     def part_wait(place, half):
-        remote(acc.at[z, halves[half]], parts.at[place, halves[half]], send_r.at[0, half], recv_r.at[place, half], at()).wait_recv()
+        remote(acc.at[z, half], parts.at[place, half], send_r.at[0, half], recv_r.at[place, half], at()).wait_recv()
 
     def peer_slot(source, target):
         return (source - target - 1 + dims) % dims
 
-    def res_copy(target, which):
-        return remote(res.at[z], res.at[z], send_g.at[which], recv_g.at[peer_slot(z, target)], at(dim=target))
+    def res_copy(target, which, half):
+        return remote(res.at[z, half], res.at[z, half], send_g.at[which, half], recv_g.at[peer_slot(z, target), half], at(dim=target))
 
     def target_at(turn):
         first, second, third = (jnp.where(outer, one, two) for one, two in ((far_outer, mate), (far_inner, far_outer), (mate, far_inner)))
@@ -163,7 +162,9 @@
                 table = jnp.broadcast_to(table, (probe.shape[0], LANES))
                 picked = jnp.take_along_axis(table, lane, axis=1, mode='promise_in_bounds')
                 got = jnp.where(page == number, picked, got)
-            cand_ids[member, :, pl.ds(pl.multiple_of(tile * LANES, LANES), LANES)] = got.astype(jnp.float32)
+            tiles_half = width // 2 // LANES
+            place = pl.ds(pl.multiple_of(tile % tiles_half * LANES, LANES), LANES)
+            cand_ids[tile // tiles_half, member, :, place] = got.astype(jnp.float32)
         return carry
 
     def list_block(step):
@@ -178,13 +179,15 @@
             low, head = probe % GROUP_LISTS, probe // GROUP_LISTS
             hits = [head == want for want in heads]
             lanes = slice(tile * LANES, (tile + 1) * LANES)
+            half, place = divmod(tile * LANES, width // 2)
+            kept_lanes = slice(place, place + LANES)
             for member in range(LIST_LEN):
-                kept = acc[part, member, :, lanes]
+                kept = acc[part, half, member, :, kept_lanes]
                 for group, hit in enumerate(hits):
                     first = group * GROUP_ROWS + member * GROUP_LISTS
                     picked = jnp.take_along_axis(scores[first:first + GROUP_LISTS, lanes], low, axis=0, mode='promise_in_bounds')
                     kept = jnp.where(hit, picked, kept)
-                acc[part, member, :, lanes] = kept
+                acc[part, half, member, :, kept_lanes] = kept
 
     def heads_at(step):
         local = step < 2 * block_steps
@@ -199,14 +202,22 @@
 
     last = 2 * block_steps + chunks // 2 - 1
 
+    spare_copy = remote(piece(chunks // 2 * other_x + (chunks - 1) // 2, chunks - 1), slot(chunks - 1, 1),
+                        send_x.at[chunks - 1], recv_x.at[chunks - 1], at(shard=across))
+
     def pass_y(chunk):
         y_copy(chunk).wait_recv()
-        x_copy(chunk).start()
+        if not (isinstance(chunk, int) and chunk == chunks - 1):
+            x_copy(chunk).start()
         dy_copy(chunk).start()
 
         @pl.when(chunk + window < chunks)
         def _():
             y_copy(chunk + window).start()
+
+        @pl.when(chunk + window == chunks)
+        def _():
+            spare_copy.start()
 
     def pass_x(chunk):
         x_copy(chunk).wait_recv()
@@ -226,13 +237,9 @@
     def early(step, carry):
         own_copy(block_at(step)).start()
 
-        @pl.when(step >= 2)
-        def _():
-            pass_y(jnp.where(step <= 5, step - 2, step - 1))
-
-        @pl.when(step == 5)
-        def _():
-            pass_y(4)
+        @pl.when(step >= 1)
+        def _():
+            pass_y(step - 1)
 
         @pl.when(step >= 5)
         def _():
@@ -262,10 +269,10 @@
 
     late_plan = {
         last - 5: 'y25 x21 x22',
-        last - 4: 'y26 y27 x23',
-        last - 3: 'y28 y29 x24 x25 y30',
-        last - 2: 'y31 x26 x27',
-        last - 1: 'x28 x29 x30',
+        last - 4: 'y26 x23 y27 x24',
+        last - 3: 'y28 x25 y29 x26',
+        last - 2: 'y30 x27 y31 x28',
+        last - 1: 'x31 x29',
     }
 
     def late(step, carry):
@@ -280,6 +287,7 @@
             for which, peer in enumerate((twin, across, far)):
                 remote(ids_ref, ids_all.at[peer], send_i.at[which], recv_i.at[which], at(shard=peer)).wait_recv()
             lax.fori_loop(0, width // LANES, name_candidates, 0)
+            pass_x(chunks - 2)
         await_step(step)
         score_all(step)
         return carry
@@ -287,15 +295,24 @@
     lax.fori_loop(0, block_steps - 1, early, 0)
     lax.fori_loop(block_steps - 1, last - 5, middle, 0)
     lax.fori_loop(last - 5, last, late, 0)
-    pass_x(chunks - 1)
     await_step(jnp.int32(last))
     last_heads = heads_at(jnp.int32(last))
 
     def finish(turn, carry):
-        @pl.when((turn > 0) & (outer | (turn == 1)))
+        @pl.when(outer & (turn == 1))
+        def _():
+            part_copy(far_outer, 0, 0, 0).start()
+
+        @pl.when(outer & (turn == 2))
+        def _():
+            part_copy(far_inner, 1, 1, 0).start()
+            part_copy(far_outer, 0, 0, 1).start()
+            part_copy(far_inner, 1, 1, 1).start()
+
+        @pl.when(jnp.where(outer, turn == 3, turn == 1))
         def _():
             for half in range(2):
-                part_copy(target_at(turn - 1), jnp.where(outer, turn - 1, 2), turn - 1, half).start()
+                part_copy(mate, 2, jnp.where(outer, 2, 0), half).start()
         score(jnp.int32(last), last_heads, target_at(turn))
         return carry
 
@@ -303,37 +320,11 @@
 
     @pl.when(jnp.logical_not(outer))
     def _():
-        for merge, target in enumerate((far_outer, far_inner)):
-            for half in range(2):
+        for half in range(2):
+            for merge, target in enumerate((far_outer, far_inner)):
                 part_wait(merge, half)
-                parts[merge, halves[half]] += acc[target, halves[half]]
+                parts[merge, half] += acc[target, half]
                 merged_copy(merge, half).start()
-
-    for place in (2, 3):
-        for half in range(2):
-            part_wait(place, half)
-
-    tiles = width // LANES
-    scores, names = [], []
-    for member in range(LIST_LEN):
-        total = acc[z, member]
-        total = total + parts[2, member] + parts[3, member]
-        name = cand_ids[member]
-        real = name >= 0.0
-        scores.append(jnp.where(real, total, -jnp.inf))
-        names.append(jnp.where(real, name, BIG))
-    for place in range(TOP_K):
-        best = functools.reduce(jnp.maximum, scores)
-        best = jnp.max(best, axis=0, keepdims=True)
-        tied = [jnp.where(score_j == best, name_j, BIG) for score_j, name_j in zip(scores, names)]
-        first = jnp.min(functools.reduce(jnp.minimum, tied), axis=0, keepdims=True)
-        for tile in range(tiles):
-            lanes = slice(tile * LANES, (tile + 1) * LANES)
-            line = place * tiles + tile
-            res[z, line:line + 1, :] = best[:, lanes]
-            res[z, TOP_K * tiles + line:TOP_K * tiles + line + 1, :] = first[:, lanes]
-        if place + 1 < TOP_K:
-            scores = [jnp.where(name_j == first, -jnp.inf, score_j) for score_j, name_j in zip(scores, names)]
 
     def drain_local(block, carry):
         own_copy(block).wait_send()
@@ -346,30 +337,58 @@
         dx_copy(chunk).wait_send()
         return carry
 
-    lax.fori_loop(0, block_steps, drain_local, 0)
+    tiles = width // 2 // LANES
+    for half in range(2):
+        for place in (2, 3):
+            part_wait(place, half)
+        scores, names = [], []
+        for member in range(LIST_LEN):
+            total = acc[z, half, member] + parts[2, half, member] + parts[3, half, member]
+            name = cand_ids[half, member]
+            real = name >= 0.0
+            scores.append(jnp.where(real, total, -jnp.inf))
+            names.append(jnp.where(real, name, BIG))
+        for place in range(TOP_K):
+            best = functools.reduce(jnp.maximum, scores)
+            best = jnp.max(best, axis=0, keepdims=True)
+            tied = [jnp.where(score_j == best, name_j, BIG) for score_j, name_j in zip(scores, names)]
+            first = jnp.min(functools.reduce(jnp.minimum, tied), axis=0, keepdims=True)
+            for tile in range(tiles):
+                lanes = slice(tile * LANES, (tile + 1) * LANES)
+                line = place * tiles + tile
+                res[z, half, line:line + 1, :] = best[:, lanes]
+                res[z, half, TOP_K * tiles + line:TOP_K * tiles + line + 1, :] = first[:, lanes]
+            if place + 1 < TOP_K:
+                scores = [jnp.where(name_j == first, -jnp.inf, score_j) for score_j, name_j in zip(scores, names)]
+        if half == 0:
+            lax.fori_loop(0, block_steps, drain_local, 0)
+        else:
+            for which, peer in enumerate((twin, across, far)):
+                id_copy(which, peer).wait_send()
+        for which in range(dims - 1):
+            res_copy(target_at(which), which, half).start()
+
     lax.fori_loop(0, chunks, drain_chunks, 0)
-    for which, peer in enumerate((twin, across, far)):
-        id_copy(which, peer).wait_send()
     for which in range(3):
         for half in range(2):
             part_copy(z, 2, which, half).wait_send()
-
     for which in range(dims - 1):
-        res_copy(target_at(which), which).start()
+        for half in range(2):
+            remote(res.at[z, half], res.at[z, half], send_g.at[which, half], recv_g.at[which, half], at()).wait_recv()
     for which in range(dims - 1):
-        remote(res.at[z], res.at[(z + 1 + which) % dims], send_g.at[which], recv_g.at[which], at()).wait_recv()
-    for which in range(dims - 1):
-        res_copy(target_at(which), which).wait_send()
+        for half in range(2):
+            res_copy(target_at(which), which, half).wait_send()
 
 
 def place_kernel(res, out_s, out_i):
-    dims, lines, _ = res.shape
+    dims, halves, lines, _ = res.shape
     tiles = lines // (2 * TOP_K)
     for part in range(dims):
-        for tile in range(tiles):
-            first = (part * tiles + tile) * LANES
-            out_s[:, first:first + LANES] = res[part, pl.ds(tile, TOP_K, stride=tiles), :]
-            out_i[:, first:first + LANES] = res[part, pl.ds(TOP_K * tiles + tile, TOP_K, stride=tiles), :].astype(jnp.int32)
+        for half in range(halves):
+            for tile in range(tiles):
+                first = ((part * halves + half) * tiles + tile) * LANES
+                out_s[:, first:first + LANES] = res[part, half, pl.ds(tile, TOP_K, stride=tiles), :]
+                out_i[:, first:first + LANES] = res[part, half, pl.ds(TOP_K * tiles + tile, TOP_K, stride=tiles), :].astype(jnp.int32)
 
 
 def solution(mesh):
@@ -389,7 +408,7 @@
         vmem_spec = pl.BlockSpec(memory_space=pltpu.VMEM)
         found = pl.pallas_call(
             functools.partial(search_kernel, dims),
-            out_shape=pltpu.VMEM((dims, 2 * TOP_K * width // LANES, LANES), jnp.float32),
+            out_shape=pltpu.VMEM((dims, 2, TOP_K * width // LANES, LANES), jnp.float32),
             in_specs=[any_spec] * 4,
             out_specs=vmem_spec,
             scratch_shapes=[
@@ -397,10 +416,10 @@
                 pltpu.VMEM((rows_q, depth), jnp.bfloat16),
                 pltpu.VMEM((4 * block_rows, depth), jnp.bfloat16),
                 pltpu.VMEM((STEP_ROWS, STEP_ROWS), jnp.bfloat16),
-                pltpu.VMEM((dims, LIST_LEN, probe_count, width), jnp.float32),
-                pltpu.VMEM((4, LIST_LEN, probe_count, width), jnp.float32),
+                pltpu.VMEM((dims, 2, LIST_LEN, probe_count, width // 2), jnp.float32),
+                pltpu.VMEM((4, 2, LIST_LEN, probe_count, width // 2), jnp.float32),
                 pltpu.VMEM((4, LIST_LEN, lists_dev), jnp.int32),
-                pltpu.VMEM((LIST_LEN, probe_count, width), jnp.float32),
+                pltpu.VMEM((2, LIST_LEN, probe_count, width // 2), jnp.float32),
                 pltpu.VMEM((probe_count, rows_q), jnp.int32),
                 pltpu.VMEM((LIST_LEN, lists_dev), jnp.int32),
                 dma, dma,
@@ -409,7 +428,7 @@
                 dma((chunks,)), dma((chunks,)), dma((chunks,)), dma((chunks,)),
                 dma((chunks,)), dma((chunks,)), dma((chunks,)), dma((chunks,)),
                 dma((3,)), dma((3,)),
-                dma((3, 2)), dma((4, 2)), dma((dims - 1,)), dma((dims - 1,)),
+                dma((3, 2)), dma((4, 2)), dma((dims - 1, 2)), dma((dims - 1, 2)),
             ],
             compiler_params=pltpu.CompilerParams(collective_id=0, has_side_effects=True, vmem_limit_bytes=60 * 2**20),
             name='ivf_search',

time: 81 us -> 80.1 us (0.989)
    pallas_call x1, Pallas kernels: 79.5 us -> 78.6 us  [local_search(): pl.pallas_call(functools.partial(search_kernel, dims), out_shape=pltpu.VM...]
where the time goes in v6:
time: 80.1 us; the launch traced here: 80 us
  Pallas kernels  79.4 us (99%)
    pallas_call x1, Pallas kernels, local_search(): pl.pallas_call(functools.partial(search_kernel, dims), out_shape=pltpu.VM...  78.6 us

profile of v6, /device:TPU:0, one launch (start us, length us, event | category | flops | bytes accessed | tf_op | source)
XLA Modules:
  0.0 80.0 jit_solution(712057947395327357)
XLA Ops:
  0.6 78.6 %ivf_search.1.res = f32[4,2,40,128]{3,2,1,0:T(8,128)S(1)} custom-call(bf16[2048,1024]{1,0:T(8,128)(2,1)} %q_hbm.1, bf16[2048,1024]{1,0:T(8,128)(2,1)} %bitcast.5, s32[8,2048]{1,0:T(8,128)} %bitcast.6, s32[8,256]{1,0:T(8,128)} %bitcast.7), custom_call_target="tpu_custom_call" | custom-call | tf_op jit(solution)/shard_map/ivf_search/pallas_call | solution.py:409
  79.3 0.7 place.1

commit v7 on v6

--- a/solution.py
+++ b/solution.py
@@ -15,6 +15,7 @@
 STEP_ROWS = STEP_GROUPS * GROUP_ROWS
 PIECE_ROWS = GROUP_ROWS // 2
 LANES = 128
+REUSE = 16
 MESH = pl.DeviceIdType.MESH
 BIG = 1e9
 
@@ -26,8 +27,7 @@
 def search_kernel(dims, q_hbm, l_hbm, probes_hbm, ids_hbm, res,
                   raw, qv, vecs, perm, acc, parts, ids_all, cand_ids, probes_ref, ids_ref, load_p, load_i,
                   load_l, load_q, send_o, recv_o, send_y, recv_y, send_x, recv_x,
-                  send_dy, recv_dy, send_dx, recv_dx, send_i, recv_i,
-                  send_r, recv_r, send_g, recv_g):
+                  send_d, recv_d, send_i, recv_i, send_r, recv_r, send_g, recv_g):
     rows_q = qv.shape[0]
     lists_dev = ids_ref.shape[1]
     block_rows = lists_dev * LIST_LEN
@@ -49,16 +49,20 @@
         return pltpu.make_async_remote_copy(src_ref=src, dst_ref=dst, send_sem=send, recv_sem=recv,
                                             device_id=device, device_id_type=MESH)
 
+    def await_recv(buffer, semaphore):
+        remote(buffer, buffer, send_i, semaphore, at()).wait_recv()
+
+    def await_send(buffer, semaphore):
+        remote(buffer, buffer, semaphore, recv_i, at()).wait_send()
+
     def load_list(block):
         return pltpu.make_async_copy(l_hbm.at[step_rows(block)], raw.at[step_rows(block)], load_l.at[block])
 
-    def load_query(part):
-        rows = pl.ds(pl.multiple_of(part * width, width), width)
-        return pltpu.make_async_copy(q_hbm.at[rows], qv.at[rows], load_q.at[part])
+    queries_in = pltpu.make_async_copy(q_hbm, qv, load_q)
 
     def own_copy(block):
         return remote(vecs.at[step_rows(block)], vecs.at[step_rows(block_steps + block)],
-                      send_o.at[block], recv_o.at[block], at(shard=twin))
+                      send_o, recv_o.at[block], at(shard=twin))
 
     def piece(group, chunk):
         first = pl.multiple_of(group * GROUP_ROWS + chunk % 2 * PIECE_ROWS, PIECE_ROWS)
@@ -68,39 +72,36 @@
         return piece(2 * block_groups + STEP_GROUPS * (chunk // 2) + which, chunk)
 
     def y_copy(chunk):
-        return remote(piece(chunks // 2 * x + chunk // 2, chunk), slot(chunk, 0), send_y.at[chunk], recv_y.at[chunk], at(shard=across))
+        return remote(piece(chunks // 2 * x + chunk // 2, chunk), slot(chunk, 0), send_y, recv_y.at[chunk % REUSE], at(shard=across))
 
     def x_copy(chunk):
-        return remote(slot(chunk, 0), slot(chunk, 1), send_x.at[chunk], recv_x.at[chunk], at(rep=other_x))
+        return remote(slot(chunk, 0), slot(chunk, 1), send_x, recv_x.at[chunk % REUSE], at(rep=other_x))
 
     def dy_copy(chunk):
-        return remote(slot(chunk, 0), slot(chunk, 2), send_dy.at[chunk], recv_dy.at[chunk], at(shard=twin))
+        return remote(slot(chunk, 0), slot(chunk, 2), send_d, recv_d.at[chunk // 2], at(shard=twin))
 
     def dx_copy(chunk):
-        return remote(slot(chunk, 1), slot(chunk, 3), send_dx.at[chunk], recv_dx.at[chunk], at(shard=twin))
+        return remote(slot(chunk, 1), slot(chunk, 3), send_d, recv_d.at[chunk // 2], at(shard=twin))
 
     def id_copy(which, peer):
-        return remote(ids_ref, ids_all.at[s], send_i.at[which], recv_i.at[which], at(shard=peer))
+        return remote(ids_ref, ids_all.at[s], send_i, recv_i, at(shard=peer))
 
     outer = z % 3 == 0
     mate, far_outer = flip(z, 1), jnp.where(z < 2, dims - 1, 0)
     far_inner = flip(far_outer, 1)
 
-    def part_copy(target, place, which, half):
-        return remote(acc.at[target, half], parts.at[place, half], send_r.at[which, half], recv_r.at[place, half], at(dim=mate))
+    def part_copy(target, place, half):
+        return remote(acc.at[target, half], parts.at[place, half], send_r, recv_r.at[place, half], at(dim=mate))
 
     def merged_copy(merge, half):
-        return remote(parts.at[merge, half], parts.at[3, half], send_r.at[1 + merge, half], recv_r.at[3, half],
+        return remote(parts.at[merge, half], parts.at[3, half], send_r, recv_r.at[3, half],
                       at(dim=(far_outer, far_inner)[merge]))
 
     def part_wait(place, half):
-        remote(acc.at[z, half], parts.at[place, half], send_r.at[0, half], recv_r.at[place, half], at()).wait_recv()
-
-    def peer_slot(source, target):
-        return (source - target - 1 + dims) % dims
-
-    def res_copy(target, which, half):
-        return remote(res.at[z, half], res.at[z, half], send_g.at[which, half], recv_g.at[peer_slot(z, target), half], at(dim=target))
+        await_recv(parts.at[place, half], recv_r.at[place, half])
+
+    def res_copy(target, half):
+        return remote(res.at[z, half], res.at[z, half], send_g, recv_g, at(dim=target))
 
     def target_at(turn):
         first, second, third = (jnp.where(outer, one, two) for one, two in ((far_outer, mate), (far_inner, far_outer), (mate, far_inner)))
@@ -114,8 +115,7 @@
     ids_in = pltpu.make_async_copy(ids_hbm, ids_ref, load_i)
     ids_in.start()
     probes_in.start()
-    for part in range(dims):
-        load_query(part).start()
+    queries_in.start()
     for turn in range(1, block_steps):
         load_list(block_at(turn)).start()
 
@@ -147,8 +147,7 @@
         id_copy(which, peer).start()
     ids_all[s] = ids_ref[...]
     probes_in.wait()
-    for part in range(dims):
-        load_query(part).wait()
+    queries_in.wait()
 
     def name_candidates(tile, carry):
         cols = pl.ds(pl.multiple_of(z * width + tile * LANES, LANES), LANES)
@@ -203,7 +202,7 @@
     last = 2 * block_steps + chunks // 2 - 1
 
     spare_copy = remote(piece(chunks // 2 * other_x + (chunks - 1) // 2, chunks - 1), slot(chunks - 1, 1),
-                        send_x.at[chunks - 1], recv_x.at[chunks - 1], at(shard=across))
+                        send_x, recv_x.at[REUSE], at(shard=across))
 
     def pass_y(chunk):
         y_copy(chunk).wait_recv()
@@ -220,14 +219,14 @@
             spare_copy.start()
 
     def pass_x(chunk):
-        x_copy(chunk).wait_recv()
+        if isinstance(chunk, int) and chunk == chunks - 1:
+            spare_copy.wait_recv()
+        else:
+            x_copy(chunk).wait_recv()
         dx_copy(chunk).start()
 
     def await_step(step):
-        first = 2 * (step - 2 * block_steps)
-        for chunk in (first, first + 1):
-            dy_copy(chunk).wait_recv()
-            dx_copy(chunk).wait_recv()
+        await_recv(vecs.at[pl.ds(0, 4 * PIECE_ROWS)], recv_d.at[step - 2 * block_steps])
 
     def score_all(step):
         heads = heads_at(step)
@@ -284,8 +283,7 @@
 
         @pl.when(step == last - 1)
         def _():
-            for which, peer in enumerate((twin, across, far)):
-                remote(ids_ref, ids_all.at[peer], send_i.at[which], recv_i.at[which], at(shard=peer)).wait_recv()
+            await_recv(ids_all.at[pl.ds(0, 3)], recv_i)
             lax.fori_loop(0, width // LANES, name_candidates, 0)
             pass_x(chunks - 2)
         await_step(step)
@@ -301,18 +299,18 @@
     def finish(turn, carry):
         @pl.when(outer & (turn == 1))
         def _():
-            part_copy(far_outer, 0, 0, 0).start()
+            part_copy(far_outer, 0, 0).start()
 
         @pl.when(outer & (turn == 2))
         def _():
-            part_copy(far_inner, 1, 1, 0).start()
-            part_copy(far_outer, 0, 0, 1).start()
-            part_copy(far_inner, 1, 1, 1).start()
+            part_copy(far_inner, 1, 0).start()
+            part_copy(far_outer, 0, 1).start()
+            part_copy(far_inner, 1, 1).start()
 
         @pl.when(jnp.where(outer, turn == 3, turn == 1))
         def _():
             for half in range(2):
-                part_copy(mate, 2, jnp.where(outer, 2, 0), half).start()
+                part_copy(mate, 2, half).start()
         score(jnp.int32(last), last_heads, target_at(turn))
         return carry
 
@@ -325,17 +323,6 @@
                 part_wait(merge, half)
                 parts[merge, half] += acc[target, half]
                 merged_copy(merge, half).start()
-
-    def drain_local(block, carry):
-        own_copy(block).wait_send()
-        return carry
-
-    def drain_chunks(chunk, carry):
-        y_copy(chunk).wait_send()
-        x_copy(chunk).wait_send()
-        dy_copy(chunk).wait_send()
-        dx_copy(chunk).wait_send()
-        return carry
 
     tiles = width // 2 // LANES
     for half in range(2):
@@ -361,23 +348,18 @@
             if place + 1 < TOP_K:
                 scores = [jnp.where(name_j == first, -jnp.inf, score_j) for score_j, name_j in zip(scores, names)]
         if half == 0:
-            lax.fori_loop(0, block_steps, drain_local, 0)
+            await_send(vecs.at[pl.ds(0, block_rows)], send_o)
+            await_send(ids_all.at[pl.ds(0, 3)], send_i)
         else:
-            for which, peer in enumerate((twin, across, far)):
-                id_copy(which, peer).wait_send()
+            await_send(vecs.at[pl.ds(0, chunks * PIECE_ROWS)], send_y)
+            await_send(vecs.at[pl.ds(0, chunks * PIECE_ROWS)], send_x)
+            await_send(vecs.at[pl.ds(0, 2 * chunks * PIECE_ROWS)], send_d)
         for which in range(dims - 1):
-            res_copy(target_at(which), which, half).start()
-
-    lax.fori_loop(0, chunks, drain_chunks, 0)
-    for which in range(3):
-        for half in range(2):
-            part_copy(z, 2, which, half).wait_send()
-    for which in range(dims - 1):
-        for half in range(2):
-            remote(res.at[z, half], res.at[z, half], send_g.at[which, half], recv_g.at[which, half], at()).wait_recv()
-    for which in range(dims - 1):
-        for half in range(2):
-            res_copy(target_at(which), which, half).wait_send()
+            res_copy(target_at(which), half).start()
+
+    await_send(parts.at[pl.ds(0, 3)], send_r)
+    await_send(res.at[pl.ds(0, dims - 1)], send_g)
+    await_recv(res.at[pl.ds(0, dims - 1)], recv_g)
 
 
 def place_kernel(res, out_s, out_i):
@@ -423,12 +405,11 @@
                 pltpu.VMEM((probe_count, rows_q), jnp.int32),
                 pltpu.VMEM((LIST_LEN, lists_dev), jnp.int32),
                 dma, dma,
-                dma((block_steps,)), dma((dims,)),
-                dma((block_steps,)), dma((block_steps,)),
-                dma((chunks,)), dma((chunks,)), dma((chunks,)), dma((chunks,)),
-                dma((chunks,)), dma((chunks,)), dma((chunks,)), dma((chunks,)),
-                dma((3,)), dma((3,)),
-                dma((3, 2)), dma((4, 2)), dma((dims - 1, 2)), dma((dims - 1, 2)),
+                dma((block_steps,)), dma,
+                dma, dma((block_steps,)),
+                dma, dma((REUSE,)), dma, dma((REUSE + 1,)),
+                dma, dma((chunks // 2,)),
+                dma, dma, dma, dma((4, 2)), dma, dma,
             ],
             compiler_params=pltpu.CompilerParams(collective_id=0, has_side_effects=True, vmem_limit_bytes=60 * 2**20),
             name='ivf_search',

time: 80.1 us -> 78.1 us (0.975)
  Pallas kernels: 79.4 us -> 77.3 us
    pallas_call x1, Pallas kernels: 78.6 us -> 76.5 us  [local_search(): pl.pallas_call(functools.partial(search_kernel, dims), out_shape=pltpu.VM...]
where the time goes in v7:
time: 78.1 us; the launch traced here: 77.9 us
  Pallas kernels  77.3 us (99%)
    pallas_call x1, Pallas kernels, local_search(): pl.pallas_call(functools.partial(search_kernel, dims), out_shape=pltpu.VM...  76.5 us

profile of v7, /device:TPU:0, one launch (start us, length us, event | category | flops | bytes accessed | tf_op | source)
XLA Modules:
  0.0 77.9 jit_solution(12198813618262544809)
XLA Ops:
  0.6 76.5 %ivf_search.1.res = f32[4,2,40,128]{3,2,1,0:T(8,128)S(1)} custom-call(bf16[2048,1024]{1,0:T(8,128)(2,1)} %q_hbm.1, bf16[2048,1024]{1,0:T(8,128)(2,1)} %bitcast.5, s32[8,2048]{1,0:T(8,128)} %bitcast.6, s32[8,256]{1,0:T(8,128)} %bitcast.7), custom_call_target="tpu_custom_call" | custom-call | tf_op jit(solution)/shard_map/ivf_search/pallas_call | solution.py:391
  77.2 0.7 place.1

commit v8 on v7

--- a/solution.py
+++ b/solution.py
@@ -110,20 +110,24 @@
     def block_at(turn):
         return (block_steps // 2 * x + turn) % block_steps
 
+    barrier = pltpu.get_barrier_semaphore()
+    peers = [at(dim=(z + hop) % dims) for hop in (2, 1, 3)]
+    peers += [at(shard=twin), at(shard=across), at(shard=far), at(rep=other_x)]
+
+    def greet(some):
+        for peer in some:
+            pl.semaphore_signal(barrier, inc=1, device_id=peer, device_id_type=MESH)
+
     load_list(block_at(0)).start()
+    greet(peers[:3])
     probes_in = pltpu.make_async_copy(probes_hbm, probes_ref, load_p)
     ids_in = pltpu.make_async_copy(ids_hbm, ids_ref, load_i)
     ids_in.start()
     probes_in.start()
     queries_in.start()
+    greet(peers[3:])
     for turn in range(1, block_steps):
         load_list(block_at(turn)).start()
-
-    barrier = pltpu.get_barrier_semaphore()
-    peers = [at(shard=twin), at(shard=across), at(shard=far), at(rep=other_x)]
-    peers += [at(dim=(z + hop) % dims) for hop in range(1, dims)]
-    for peer in peers:
-        pl.semaphore_signal(barrier, inc=1, device_id=peer, device_id_type=MESH)
 
     row = lax.broadcasted_iota(jnp.int32, (STEP_ROWS, STEP_ROWS), 0)
     col = lax.broadcasted_iota(jnp.int32, (STEP_ROWS, STEP_ROWS), 1)
@@ -296,18 +300,20 @@
     await_step(jnp.int32(last))
     last_heads = heads_at(jnp.int32(last))
 
+    leads, follows = outer & (s % 2 == 0), outer & (s % 2 == 1)
+
     def finish(turn, carry):
-        @pl.when(outer & (turn == 1))
+        @pl.when(leads & (turn == 1))
         def _():
             part_copy(far_outer, 0, 0).start()
 
-        @pl.when(outer & (turn == 2))
+        @pl.when(leads & (turn == 2))
         def _():
             part_copy(far_inner, 1, 0).start()
             part_copy(far_outer, 0, 1).start()
             part_copy(far_inner, 1, 1).start()
 
-        @pl.when(jnp.where(outer, turn == 3, turn == 1))
+        @pl.when((leads & (turn == 3)) | (jnp.logical_not(outer) & (turn == 1)))
         def _():
             for half in range(2):
                 part_copy(mate, 2, half).start()
@@ -315,6 +321,15 @@
         return carry
 
     lax.fori_loop(0, dims, finish, 0)
+
+    @pl.when(follows)
+    def _():
+        part_wait(2, 0)
+        for half in range(2):
+            part_copy(far_outer, 0, half).start()
+            part_copy(far_inner, 1, half).start()
+        for half in range(2):
+            part_copy(mate, 2, half).start()
 
     @pl.when(jnp.logical_not(outer))
     def _():
@@ -326,8 +341,13 @@
 
     tiles = width // 2 // LANES
     for half in range(2):
-        for place in (2, 3):
-            part_wait(place, half)
+        if half == 0:
+            @pl.when(jnp.logical_not(follows))
+            def _():
+                part_wait(2, 0)
+        else:
+            part_wait(2, 1)
+        part_wait(3, half)
         scores, names = [], []
         for member in range(LIST_LEN):
             total = acc[z, half, member] + parts[2, half, member] + parts[3, half, member]

time: 78.1 us -> 77.4 us (level)
  the two profiles are of different devices: /device:TPU:0 before, /device:TPU:1 now
where the time goes in v8:
time: 77.4 us; the launch traced here: 77.2 us
  Pallas kernels  76.6 us (99%)
    pallas_call x1, Pallas kernels, local_search(): pl.pallas_call(functools.partial(search_kernel, dims), out_shape=pltpu.VM...  75.9 us

profile of v8, /device:TPU:1, one launch (start us, length us, event | category | flops | bytes accessed | tf_op | source)
XLA Modules:
  0.0 77.2 jit_solution(15724907279362147816)
XLA Ops:
  0.6 75.9 %ivf_search.1.res = f32[4,2,40,128]{3,2,1,0:T(8,128)S(1)} custom-call(bf16[2048,1024]{1,0:T(8,128)(2,1)} %q_hbm.1, bf16[2048,1024]{1,0:T(8,128)(2,1)} %bitcast.5, s32[8,2048]{1,0:T(8,128)} %bitcast.6, s32[8,256]{1,0:T(8,128)} %bitcast.7), custom_call_target="tpu_custom_call" | custom-call | tf_op jit(solution)/shard_map/ivf_search/pallas_call | solution.py:411
  76.5 0.7 place.1

commit v9 on v8

--- a/solution.py
+++ b/solution.py
@@ -324,7 +324,6 @@
 
     @pl.when(follows)
     def _():
-        part_wait(2, 0)
         for half in range(2):
             part_copy(far_outer, 0, half).start()
             part_copy(far_inner, 1, half).start()
@@ -341,12 +340,7 @@
 
     tiles = width // 2 // LANES
     for half in range(2):
-        if half == 0:
-            @pl.when(jnp.logical_not(follows))
-            def _():
-                part_wait(2, 0)
-        else:
-            part_wait(2, 1)
+        part_wait(2, half)
         part_wait(3, half)
         scores, names = [], []
         for member in range(LIST_LEN):

time: 77.4 us -> 77.1 us (level)
  the two profiles are of different devices: /device:TPU:1 before, /device:TPU:0 now
where the time goes in v9:
time: 77.1 us; the launch traced here: 76.7 us
  Pallas kernels  76.1 us (99%)
    pallas_call x1, Pallas kernels, local_search(): pl.pallas_call(functools.partial(search_kernel, dims), out_shape=pltpu.VM...  75.3 us

profile of v9, /device:TPU:0, one launch (start us, length us, event | category | flops | bytes accessed | tf_op | source)
XLA Modules:
  0.0 76.7 jit_solution(14608848796233412946)
XLA Ops:
  0.6 75.3 %ivf_search.1.res = f32[4,2,40,128]{3,2,1,0:T(8,128)S(1)} custom-call(bf16[2048,1024]{1,0:T(8,128)(2,1)} %q_hbm.1, bf16[2048,1024]{1,0:T(8,128)(2,1)} %bitcast.5, s32[8,2048]{1,0:T(8,128)} %bitcast.6, s32[8,256]{1,0:T(8,128)} %bitcast.7), custom_call_target="tpu_custom_call" | custom-call | tf_op jit(solution)/shard_map/ivf_search/pallas_call | solution.py:405
  76.0 0.7 place.1

commit v10 on v9

--- a/solution.py
+++ b/solution.py
@@ -15,7 +15,7 @@
 STEP_ROWS = STEP_GROUPS * GROUP_ROWS
 PIECE_ROWS = GROUP_ROWS // 2
 LANES = 128
-REUSE = 16
+REUSE_Y, REUSE_X = 8, 12
 MESH = pl.DeviceIdType.MESH
 BIG = 1e9
 
@@ -55,14 +55,17 @@
     def await_send(buffer, semaphore):
         remote(buffer, buffer, semaphore, recv_i, at()).wait_send()
 
-    def load_list(block):
-        return pltpu.make_async_copy(l_hbm.at[step_rows(block)], raw.at[step_rows(block)], load_l.at[block])
+    def load_lists(number):
+        half = block_steps // 2
+        first, count = ((half * x, 1), (half * x + 1, half - 1), (half * other_x, half))[number]
+        rows = pl.ds(pl.multiple_of(first * STEP_ROWS, STEP_ROWS), count * STEP_ROWS)
+        return pltpu.make_async_copy(l_hbm.at[rows], raw.at[rows], load_l.at[number])
 
     queries_in = pltpu.make_async_copy(q_hbm, qv, load_q)
 
     def own_copy(block):
         return remote(vecs.at[step_rows(block)], vecs.at[step_rows(block_steps + block)],
-                      send_o, recv_o.at[block], at(shard=twin))
+                      send_o, recv_o.at[(block // (block_steps // 2) + x) % 2], at(shard=twin))
 
     def piece(group, chunk):
         first = pl.multiple_of(group * GROUP_ROWS + chunk % 2 * PIECE_ROWS, PIECE_ROWS)
@@ -72,10 +75,10 @@
         return piece(2 * block_groups + STEP_GROUPS * (chunk // 2) + which, chunk)
 
     def y_copy(chunk):
-        return remote(piece(chunks // 2 * x + chunk // 2, chunk), slot(chunk, 0), send_y, recv_y.at[chunk % REUSE], at(shard=across))
+        return remote(piece(chunks // 2 * x + chunk // 2, chunk), slot(chunk, 0), send_y, recv_y.at[chunk % REUSE_Y], at(shard=across))
 
     def x_copy(chunk):
-        return remote(slot(chunk, 0), slot(chunk, 1), send_x, recv_x.at[chunk % REUSE], at(rep=other_x))
+        return remote(slot(chunk, 0), slot(chunk, 1), send_x, recv_x.at[chunk % REUSE_X], at(rep=other_x))
 
     def dy_copy(chunk):
         return remote(slot(chunk, 0), slot(chunk, 2), send_d, recv_d.at[chunk // 2], at(shard=twin))
@@ -118,7 +121,7 @@
         for peer in some:
             pl.semaphore_signal(barrier, inc=1, device_id=peer, device_id_type=MESH)
 
-    load_list(block_at(0)).start()
+    load_lists(0).start()
     greet(peers[:3])
     probes_in = pltpu.make_async_copy(probes_hbm, probes_ref, load_p)
     ids_in = pltpu.make_async_copy(ids_hbm, ids_ref, load_i)
@@ -126,8 +129,8 @@
     probes_in.start()
     queries_in.start()
     greet(peers[3:])
-    for turn in range(1, block_steps):
-        load_list(block_at(turn)).start()
+    load_lists(1).start()
+    load_lists(2).start()
 
     row = lax.broadcasted_iota(jnp.int32, (STEP_ROWS, STEP_ROWS), 0)
     col = lax.broadcasted_iota(jnp.int32, (STEP_ROWS, STEP_ROWS), 1)
@@ -139,8 +142,8 @@
         moved = jnp.dot(perm[...], raw[step_rows(block), :], preferred_element_type=jnp.float32)
         vecs[step_rows(block), :] = moved.astype(jnp.bfloat16)
 
-    window = 2 * STEP_GROUPS
-    load_list(block_at(0)).wait()
+    window = REUSE_Y // 2
+    load_lists(0).wait()
     arrange(0)
     pl.semaphore_wait(barrier, len(peers))
     for chunk in range(window):
@@ -171,10 +174,10 @@
         return carry
 
     def list_block(step):
-        return jnp.where(step < block_steps, block_at(step), step % block_steps)
+        return block_at(step % block_steps)
 
     def score(step, heads, part):
-        lists = vecs[step_rows(jnp.where(step < block_steps, block_at(step), step)), :]
+        lists = vecs[step_rows(jnp.where(step < 2 * block_steps, step // block_steps * block_steps + list_block(step), step)), :]
         rows = pl.ds(pl.multiple_of(part * width, width), width)
         scores = lax.dot_general(lists, qv[rows, :], (((1,), (1,)), ((), ())), preferred_element_type=jnp.float32)
         for tile in range(width // LANES):
@@ -206,7 +209,7 @@
     last = 2 * block_steps + chunks // 2 - 1
 
     spare_copy = remote(piece(chunks // 2 * other_x + (chunks - 1) // 2, chunks - 1), slot(chunks - 1, 1),
-                        send_x, recv_x.at[REUSE], at(shard=across))
+                        send_x, recv_x.at[REUSE_X], at(shard=across))
 
     def pass_y(chunk):
         y_copy(chunk).wait_recv()
@@ -247,7 +250,14 @@
         @pl.when(step >= 5)
         def _():
             pass_x(step - 5)
-        load_list(block_at(step + 1)).wait()
+
+        @pl.when(step == 0)
+        def _():
+            load_lists(1).wait()
+
+        @pl.when(step == block_steps // 2 - 1)
+        def _():
+            load_lists(2).wait()
         score_all(step)
         arrange(step + 1)
         return carry
@@ -260,9 +270,9 @@
         def _():
             own_copy(block_at(step)).start()
 
-        @pl.when((step >= block_steps) & (step < 2 * block_steps))
-        def _():
-            own_copy(step - block_steps).wait_recv()
+        @pl.when((step == block_steps) | (step == block_steps + block_steps // 2))
+        def _():
+            await_recv(vecs.at[pl.ds(0, block_rows // 2)], recv_o.at[step // (block_steps // 2) - 2])
 
         @pl.when(step >= 2 * block_steps)
         def _():
@@ -273,9 +283,9 @@
     late_plan = {
         last - 5: 'y25 x21 x22',
         last - 4: 'y26 x23 y27 x24',
-        last - 3: 'y28 x25 y29 x26',
-        last - 2: 'y30 x27 y31 x28',
-        last - 1: 'x31 x29',
+        last - 3: 'y28 x25 names y29 x26',
+        last - 2: 'y30 x27 y31 x28 x29',
+        last - 1: 'x31 x30',
     }
 
     def late(step, carry):
@@ -283,13 +293,12 @@
             @pl.when(step == when)
             def _(plan=plan):
                 for word in plan.split():
-                    (pass_y if word[0] == 'y' else pass_x)(int(word[1:]))
-
-        @pl.when(step == last - 1)
-        def _():
-            await_recv(ids_all.at[pl.ds(0, 3)], recv_i)
-            lax.fori_loop(0, width // LANES, name_candidates, 0)
-            pass_x(chunks - 2)
+                    if word == 'names':
+                        await_recv(ids_all.at[pl.ds(0, 3)], recv_i)
+                        lax.fori_loop(0, width // LANES, name_candidates, 0)
+                    else:
+                        (pass_y if word[0] == 'y' else pass_x)(int(word[1:]))
+
         await_step(step)
         score_all(step)
         return carry
@@ -419,9 +428,9 @@
                 pltpu.VMEM((probe_count, rows_q), jnp.int32),
                 pltpu.VMEM((LIST_LEN, lists_dev), jnp.int32),
                 dma, dma,
-                dma((block_steps,)), dma,
-                dma, dma((block_steps,)),
-                dma, dma((REUSE,)), dma, dma((REUSE + 1,)),
+                dma((3,)), dma,
+                dma, dma((2,)),
+                dma, dma((REUSE_Y,)), dma, dma((REUSE_X + 1,)),
                 dma, dma((chunks // 2,)),
                 dma, dma, dma, dma((4, 2)), dma, dma,
             ],

time: 77.1 us -> 76.9 us (level)
  no operation moved by 1% of the time
where the time goes in v10:
time: 76.9 us; the launch traced here: 76.2 us
  Pallas kernels  75.5 us (98%)
    pallas_call x1, Pallas kernels, local_search(): pl.pallas_call(functools.partial(search_kernel, dims), out_shape=pltpu.VM...  74.8 us

profile of v10, /device:TPU:0, one launch (start us, length us, event | category | flops | bytes accessed | tf_op | source)
XLA Modules:
  0.0 76.2 jit_solution(1865191177219851593)
XLA Ops:
  0.6 74.8 %ivf_search.1.res = f32[4,2,40,128]{3,2,1,0:T(8,128)S(1)} custom-call(bf16[2048,1024]{1,0:T(8,128)(2,1)} %q_hbm.1, bf16[2048,1024]{1,0:T(8,128)(2,1)} %bitcast.5, s32[8,2048]{1,0:T(8,128)} %bitcast.6, s32[8,256]{1,0:T(8,128)} %bitcast.7), custom_call_target="tpu_custom_call" | custom-call | tf_op jit(solution)/shard_map/ivf_search/pallas_call | solution.py:414
  75.4 0.7 place.1

commit v11 on v10

--- a/solution.py
+++ b/solution.py
@@ -27,7 +27,7 @@
 def search_kernel(dims, q_hbm, l_hbm, probes_hbm, ids_hbm, res,
                   raw, qv, vecs, perm, acc, parts, ids_all, cand_ids, probes_ref, ids_ref, load_p, load_i,
                   load_l, load_q, send_o, recv_o, send_y, recv_y, send_x, recv_x,
-                  send_d, recv_d, send_i, recv_i, send_r, recv_r, send_g, recv_g):
+                  send_d, recv_d, send_i, recv_i, send_r, recv_r, send_g, recv_g, met):
     rows_q = qv.shape[0]
     lists_dev = ids_ref.shape[1]
     block_rows = lists_dev * LIST_LEN
@@ -114,21 +114,27 @@
         return (block_steps // 2 * x + turn) % block_steps
 
     barrier = pltpu.get_barrier_semaphore()
-    peers = [at(dim=(z + hop) % dims) for hop in (2, 1, 3)]
-    peers += [at(shard=twin), at(shard=across), at(shard=far), at(rep=other_x)]
-
-    def greet(some):
-        for peer in some:
-            pl.semaphore_signal(barrier, inc=1, device_id=peer, device_id_type=MESH)
+    peers = [at(shard=twin), at(shard=across), at(shard=far), at(rep=other_x)]
+    beside = jnp.where(outer, 1, 2)
+
+    def tell_line(semaphore):
+        @pl.when(z < dims - 1)
+        def _():
+            pl.semaphore_signal(semaphore, inc=1, device_id=at(dim=(z + 1) % dims), device_id_type=MESH)
+
+        @pl.when(z > 0)
+        def _():
+            pl.semaphore_signal(semaphore, inc=1, device_id=at(dim=(z + dims - 1) % dims), device_id_type=MESH)
 
     load_lists(0).start()
-    greet(peers[:3])
+    tell_line(barrier)
     probes_in = pltpu.make_async_copy(probes_hbm, probes_ref, load_p)
     ids_in = pltpu.make_async_copy(ids_hbm, ids_ref, load_i)
     ids_in.start()
     probes_in.start()
     queries_in.start()
-    greet(peers[3:])
+    for peer in peers:
+        pl.semaphore_signal(barrier, inc=1, device_id=peer, device_id_type=MESH)
     load_lists(1).start()
     load_lists(2).start()
 
@@ -145,9 +151,10 @@
     window = REUSE_Y // 2
     load_lists(0).wait()
     arrange(0)
-    pl.semaphore_wait(barrier, len(peers))
+    pl.semaphore_wait(barrier, len(peers) + beside)
     for chunk in range(window):
         y_copy(chunk).start()
+    tell_line(met.at[0])
     acc[...] = jnp.zeros_like(acc)
     ids_in.wait()
     for which, peer in enumerate((twin, across, far)):
@@ -305,7 +312,10 @@
 
     lax.fori_loop(0, block_steps - 1, early, 0)
     lax.fori_loop(block_steps - 1, last - 5, middle, 0)
+    pl.semaphore_wait(met.at[0], beside)
+    tell_line(met.at[1])
     lax.fori_loop(last - 5, last, late, 0)
+    pl.semaphore_wait(met.at[1], beside)
     await_step(jnp.int32(last))
     last_heads = heads_at(jnp.int32(last))
 
@@ -433,6 +443,7 @@
                 dma, dma((REUSE_Y,)), dma, dma((REUSE_X + 1,)),
                 dma, dma((chunks // 2,)),
                 dma, dma, dma, dma((4, 2)), dma, dma,
+                pltpu.SemaphoreType.REGULAR((2,)),
             ],
             compiler_params=pltpu.CompilerParams(collective_id=0, has_side_effects=True, vmem_limit_bytes=60 * 2**20),
             name='ivf_search',

time: 76.9 us -> 76.2 us (level)
  no operation moved by 1% of the time
where the time goes in v11:
time: 76.2 us; the launch traced here: 75.4 us
  Pallas kernels  74.8 us (98%)
    pallas_call x1, Pallas kernels, local_search(): pl.pallas_call(functools.partial(search_kernel, dims), out_shape=pltpu.VM...  74 us

profile of v11, /device:TPU:0, one launch (start us, length us, event | category | flops | bytes accessed | tf_op | source)
XLA Modules:
  0.0 75.4 jit_solution(16838054030073973414)
XLA Ops:
  0.6 74.0 %ivf_search.1.res = f32[4,2,40,128]{3,2,1,0:T(8,128)S(1)} custom-call(bf16[2048,1024]{1,0:T(8,128)(2,1)} %q_hbm.1, bf16[2048,1024]{1,0:T(8,128)(2,1)} %bitcast.5, s32[8,2048]{1,0:T(8,128)} %bitcast.6, s32[8,256]{1,0:T(8,128)} %bitcast.7), custom_call_target="tpu_custom_call" | custom-call | tf_op jit(solution)/shard_map/ivf_search/pallas_call | solution.py:424
  74.7 0.7 place.1

commit v12 on v11

--- a/solution.py
+++ b/solution.py
@@ -288,18 +288,18 @@
         return carry
 
     late_plan = {
-        last - 5: 'y25 x21 x22',
-        last - 4: 'y26 x23 y27 x24',
-        last - 3: 'y28 x25 names y29 x26',
-        last - 2: 'y30 x27 y31 x28 x29',
-        last - 1: 'x31 x30',
+        last - 5: ('y25', 'x21', 'x22'),
+        last - 4: ('y26', 'x23', 'y27', 'x24'),
+        last - 3: ('y28', 'x25', 'names', 'y29', 'x26'),
+        last - 2: ('y30', 'x27', 'y31', 'x28', 'x29'),
+        last - 1: ('x31', 'x30'),
     }
 
     def late(step, carry):
         for when, plan in late_plan.items():
             @pl.when(step == when)
             def _(plan=plan):
-                for word in plan.split():
+                for word in plan:
                     if word == 'names':
                         await_recv(ids_all.at[pl.ds(0, 3)], recv_i)
                         lax.fori_loop(0, width // LANES, name_candidates, 0)

time: 76.2 us -> 76.2 us (level)
  no operation moved by 1% of the time
where the time goes in v12:
time: 76.2 us; the launch traced here: 75.4 us
  Pallas kernels  74.8 us (98%)
    pallas_call x1, Pallas kernels, local_search(): pl.pallas_call(functools.partial(search_kernel, dims), out_shape=pltpu.VM...  74 us

profile of v12, /device:TPU:0, one launch (start us, length us, event | category | flops | bytes accessed | tf_op | source)
XLA Modules:
  0.0 75.4 jit_solution(16838054030073973414)
XLA Ops:
  0.6 74.0 %ivf_search.1.res = f32[4,2,40,128]{3,2,1,0:T(8,128)S(1)} custom-call(bf16[2048,1024]{1,0:T(8,128)(2,1)} %q_hbm.1, bf16[2048,1024]{1,0:T(8,128)(2,1)} %bitcast.5, s32[8,2048]{1,0:T(8,128)} %bitcast.6, s32[8,256]{1,0:T(8,128)} %bitcast.7), custom_call_target="tpu_custom_call" | custom-call | tf_op jit(solution)/shard_map/ivf_search/pallas_call | solution.py:424
  74.7 0.7 place.1

commit v13 on v12

--- a/solution.py
+++ b/solution.py
@@ -35,6 +35,8 @@
     chunks = block_groups
     block_steps = block_groups // STEP_GROUPS
     width = rows_q // dims
+    row_blocks = 2 * dims
+    block_width = rows_q // row_blocks
     x, z, s = lax.axis_index('rep'), lax.axis_index('dim'), lax.axis_index('shard')
     twin, across, far = flip(s, 1), flip(s, 2), flip(flip(s, 1), 2)
     other_x = 1 - x
@@ -89,26 +91,36 @@
     def id_copy(which, peer):
         return remote(ids_ref, ids_all.at[s], send_i, recv_i, at(shard=peer))
 
-    outer = z % 3 == 0
-    mate, far_outer = flip(z, 1), jnp.where(z < 2, dims - 1, 0)
+    outer, low = z % 3 == 0, z < 2
+    mate, far_outer = flip(z, 1), jnp.where(low, dims - 1, 0)
     far_inner = flip(far_outer, 1)
-
-    def part_copy(target, place, half):
-        return remote(acc.at[target, half], parts.at[place, half], send_r, recv_r.at[place, half], at(dim=mate))
-
-    def merged_copy(merge, half):
-        return remote(parts.at[merge, half], parts.at[3, half], send_r, recv_r.at[3, half],
-                      at(dim=(far_outer, far_inner)[merge]))
-
-    def part_wait(place, half):
-        await_recv(parts.at[place, half], recv_r.at[place, half])
-
-    def res_copy(target, half):
-        return remote(res.at[z, half], res.at[z, half], send_g, recv_g, at(dim=target))
+    owned = jnp.where(outer, 3, 1)
+
+    def mirrored(block):
+        return jnp.where(low, block, row_blocks - 1 - block)
+
+    def owned_block(turn):
+        return mirrored(jnp.where(outer, (turn + 2) % 3, 3))
+
+    def part_copy(block, place):
+        return remote(acc.at[block], parts.at[place], send_r, recv_r.at[place], at(dim=mate))
+
+    def merged_copy(merge):
+        target, place = (far_inner, 5) if merge == 0 else (far_outer, 2 + merge)
+        return remote(parts.at[merge], parts.at[place], send_r, recv_r.at[place], at(dim=target))
+
+    def part_wait(place):
+        await_recv(parts.at[place], recv_r.at[place])
+
+    def res_copy(block, turn, hop):
+        return remote(res.at[block], res.at[block], send_g.at[turn], recv_g, at(dim=(z + hop) % dims))
 
     def target_at(turn):
-        first, second, third = (jnp.where(outer, one, two) for one, two in ((far_outer, mate), (far_inner, far_outer), (mate, far_inner)))
-        return jnp.where(turn == 0, first, jnp.where(turn == 1, second, jnp.where(turn == 2, third, z)))
+        return jnp.where(low, quarter_order(turn), dims - 1 - quarter_order(turn))
+
+    def quarter_order(turn):
+        first, second, third, fourth = (jnp.where(outer, one, two) for one, two in ((2, 1), (1, 0), (3, 2), (0, 3)))
+        return jnp.where(turn == 0, first, jnp.where(turn == 1, second, jnp.where(turn == 2, third, fourth)))
 
     def block_at(turn):
         return (block_steps // 2 * x + turn) % block_steps
@@ -163,8 +175,11 @@
     probes_in.wait()
     queries_in.wait()
 
-    def name_candidates(tile, carry):
-        cols = pl.ds(pl.multiple_of(z * width + tile * LANES, LANES), LANES)
+    tiles = block_width // LANES
+
+    def name_candidates(number, carry):
+        turn, tile = number // tiles, number % tiles
+        cols = pl.ds(pl.multiple_of(owned_block(turn) * block_width + tile * LANES, LANES), LANES)
         probe = probes_ref[:, cols]
         lane, page = probe % LANES, probe // LANES
         pages = lists_dev // LANES
@@ -175,9 +190,7 @@
                 table = jnp.broadcast_to(table, (probe.shape[0], LANES))
                 picked = jnp.take_along_axis(table, lane, axis=1, mode='promise_in_bounds')
                 got = jnp.where(page == number, picked, got)
-            tiles_half = width // 2 // LANES
-            place = pl.ds(pl.multiple_of(tile % tiles_half * LANES, LANES), LANES)
-            cand_ids[tile // tiles_half, member, :, place] = got.astype(jnp.float32)
+            cand_ids[turn, member, :, pl.ds(pl.multiple_of(tile * LANES, LANES), LANES)] = got.astype(jnp.float32)
         return carry
 
     def list_block(step):
@@ -192,15 +205,15 @@
             low, head = probe % GROUP_LISTS, probe // GROUP_LISTS
             hits = [head == want for want in heads]
             lanes = slice(tile * LANES, (tile + 1) * LANES)
-            half, place = divmod(tile * LANES, width // 2)
+            half, place = divmod(tile * LANES, block_width)
             kept_lanes = slice(place, place + LANES)
             for member in range(LIST_LEN):
-                kept = acc[part, half, member, :, kept_lanes]
+                kept = acc[2 * part + half, member, :, kept_lanes]
                 for group, hit in enumerate(hits):
                     first = group * GROUP_ROWS + member * GROUP_LISTS
                     picked = jnp.take_along_axis(scores[first:first + GROUP_LISTS, lanes], low, axis=0, mode='promise_in_bounds')
                     kept = jnp.where(hit, picked, kept)
-                acc[part, half, member, :, kept_lanes] = kept
+                acc[2 * part + half, member, :, kept_lanes] = kept
 
     def heads_at(step):
         local = step < 2 * block_steps
@@ -302,7 +315,7 @@
                 for word in plan:
                     if word == 'names':
                         await_recv(ids_all.at[pl.ds(0, 3)], recv_i)
-                        lax.fori_loop(0, width // LANES, name_candidates, 0)
+                        lax.fori_loop(0, owned * tiles, name_candidates, 0)
                     else:
                         (pass_y if word[0] == 'y' else pass_x)(int(word[1:]))
 
@@ -320,22 +333,22 @@
     last_heads = heads_at(jnp.int32(last))
 
     leads, follows = outer & (s % 2 == 0), outer & (s % 2 == 1)
+    outer_sends = ((4, 0), (5, 1), (3, 4), (7, 2), (6, 3))
+    inner_sends = ((2, 0), (0, 1), (1, 2))
+
+    def send_parts(plan):
+        for block, place in plan:
+            part_copy(mirrored(block), place).start()
 
     def finish(turn, carry):
-        @pl.when(leads & (turn == 1))
-        def _():
-            part_copy(far_outer, 0, 0).start()
-
-        @pl.when(leads & (turn == 2))
-        def _():
-            part_copy(far_inner, 1, 0).start()
-            part_copy(far_outer, 0, 1).start()
-            part_copy(far_inner, 1, 1).start()
-
-        @pl.when((leads & (turn == 3)) | (jnp.logical_not(outer) & (turn == 1)))
-        def _():
-            for half in range(2):
-                part_copy(mate, 2, half).start()
+        for when, some in ((1, outer_sends[:2]), (2, outer_sends[2:3]), (3, outer_sends[3:])):
+            @pl.when(leads & (turn == when))
+            def _(some=some):
+                send_parts(some)
+        for when, some in ((1, inner_sends[:1]), (2, inner_sends[1:])):
+            @pl.when(jnp.logical_not(outer) & (turn == when))
+            def _(some=some):
+                send_parts(some)
         score(jnp.int32(last), last_heads, target_at(turn))
         return carry
 
@@ -343,28 +356,30 @@
 
     @pl.when(follows)
     def _():
-        for half in range(2):
-            part_copy(far_outer, 0, half).start()
-            part_copy(far_inner, 1, half).start()
-        for half in range(2):
-            part_copy(mate, 2, half).start()
+        send_parts(outer_sends)
 
     @pl.when(jnp.logical_not(outer))
     def _():
-        for half in range(2):
-            for merge, target in enumerate((far_outer, far_inner)):
-                part_wait(merge, half)
-                parts[merge, half] += acc[target, half]
-                merged_copy(merge, half).start()
-
-    tiles = width // 2 // LANES
-    for half in range(2):
-        part_wait(2, half)
-        part_wait(3, half)
+        for merge, block in enumerate((4, 5, 7, 6)):
+            part_wait(merge)
+            parts[merge] += acc[mirrored(block)]
+            merged_copy(merge).start()
+
+    await_send(vecs.at[pl.ds(0, block_rows)], send_o)
+    await_send(ids_all.at[pl.ds(0, 3)], send_i)
+    await_send(vecs.at[pl.ds(0, chunks * PIECE_ROWS)], send_y)
+    await_send(vecs.at[pl.ds(0, chunks * PIECE_ROWS)], send_x)
+    await_send(vecs.at[pl.ds(0, 2 * chunks * PIECE_ROWS)], send_d)
+
+    def choose(turn, carry):
+        near, cross = jnp.where(outer, turn, 4), jnp.where(outer, 3 + turn, 5)
+        part_wait(near)
+        part_wait(cross)
+        block = owned_block(turn)
         scores, names = [], []
         for member in range(LIST_LEN):
-            total = acc[z, half, member] + parts[2, half, member] + parts[3, half, member]
-            name = cand_ids[half, member]
+            total = acc[block, member] + parts[near, member] + parts[cross, member]
+            name = cand_ids[turn, member]
             real = name >= 0.0
             scores.append(jnp.where(real, total, -jnp.inf))
             names.append(jnp.where(real, name, BIG))
@@ -376,34 +391,41 @@
             for tile in range(tiles):
                 lanes = slice(tile * LANES, (tile + 1) * LANES)
                 line = place * tiles + tile
-                res[z, half, line:line + 1, :] = best[:, lanes]
-                res[z, half, TOP_K * tiles + line:TOP_K * tiles + line + 1, :] = first[:, lanes]
+                res[block, line:line + 1, :] = best[:, lanes]
+                res[block, TOP_K * tiles + line:TOP_K * tiles + line + 1, :] = first[:, lanes]
             if place + 1 < TOP_K:
                 scores = [jnp.where(name_j == first, -jnp.inf, score_j) for score_j, name_j in zip(scores, names)]
-        if half == 0:
-            await_send(vecs.at[pl.ds(0, block_rows)], send_o)
-            await_send(ids_all.at[pl.ds(0, 3)], send_i)
-        else:
-            await_send(vecs.at[pl.ds(0, chunks * PIECE_ROWS)], send_y)
-            await_send(vecs.at[pl.ds(0, chunks * PIECE_ROWS)], send_x)
-            await_send(vecs.at[pl.ds(0, 2 * chunks * PIECE_ROWS)], send_d)
-        for which in range(dims - 1):
-            res_copy(target_at(which), half).start()
-
-    await_send(parts.at[pl.ds(0, 3)], send_r)
-    await_send(res.at[pl.ds(0, dims - 1)], send_g)
-    await_recv(res.at[pl.ds(0, dims - 1)], recv_g)
+        for hop in (2, 1, 3):
+            res_copy(block, turn, hop).start()
+        return carry
+
+    lax.fori_loop(0, owned, choose, 0)
+
+    def drain(turn, carry):
+        await_send(res.at[pl.ds(0, dims - 1)], send_g.at[turn])
+        return carry
+
+    lax.fori_loop(0, owned, drain, 0)
+
+    @pl.when(outer)
+    def _():
+        await_send(acc.at[pl.ds(0, 5)], send_r)
+        await_recv(res.at[pl.ds(0, 5)], recv_g)
+
+    @pl.when(jnp.logical_not(outer))
+    def _():
+        await_send(acc.at[pl.ds(0, 7)], send_r)
+        await_recv(res.at[pl.ds(0, 7)], recv_g)
 
 
 def place_kernel(res, out_s, out_i):
-    dims, halves, lines, _ = res.shape
+    blocks, lines, _ = res.shape
     tiles = lines // (2 * TOP_K)
-    for part in range(dims):
-        for half in range(halves):
-            for tile in range(tiles):
-                first = ((part * halves + half) * tiles + tile) * LANES
-                out_s[:, first:first + LANES] = res[part, half, pl.ds(tile, TOP_K, stride=tiles), :]
-                out_i[:, first:first + LANES] = res[part, half, pl.ds(TOP_K * tiles + tile, TOP_K, stride=tiles), :].astype(jnp.int32)
+    for block in range(blocks):
+        for tile in range(tiles):
+            first = (block * tiles + tile) * LANES
+            out_s[:, first:first + LANES] = res[block, pl.ds(tile, TOP_K, stride=tiles), :]
+            out_i[:, first:first + LANES] = res[block, pl.ds(TOP_K * tiles + tile, TOP_K, stride=tiles), :].astype(jnp.int32)
 
 
 def solution(mesh):
@@ -423,7 +445,7 @@
         vmem_spec = pl.BlockSpec(memory_space=pltpu.VMEM)
         found = pl.pallas_call(
             functools.partial(search_kernel, dims),
-            out_shape=pltpu.VMEM((dims, 2, TOP_K * width // LANES, LANES), jnp.float32),
+            out_shape=pltpu.VMEM((2 * dims, TOP_K * width // LANES, LANES), jnp.float32),
             in_specs=[any_spec] * 4,
             out_specs=vmem_spec,
             scratch_shapes=[
@@ -431,10 +453,10 @@
                 pltpu.VMEM((rows_q, depth), jnp.bfloat16),
                 pltpu.VMEM((4 * block_rows, depth), jnp.bfloat16),
                 pltpu.VMEM((STEP_ROWS, STEP_ROWS), jnp.bfloat16),
-                pltpu.VMEM((dims, 2, LIST_LEN, probe_count, width // 2), jnp.float32),
-                pltpu.VMEM((4, 2, LIST_LEN, probe_count, width // 2), jnp.float32),
+                pltpu.VMEM((2 * dims, LIST_LEN, probe_count, width // 2), jnp.float32),
+                pltpu.VMEM((6, LIST_LEN, probe_count, width // 2), jnp.float32),
                 pltpu.VMEM((4, LIST_LEN, lists_dev), jnp.int32),
-                pltpu.VMEM((2, LIST_LEN, probe_count, width // 2), jnp.float32),
+                pltpu.VMEM((3, LIST_LEN, probe_count, width // 2), jnp.float32),
                 pltpu.VMEM((probe_count, rows_q), jnp.int32),
                 pltpu.VMEM((LIST_LEN, lists_dev), jnp.int32),
                 dma, dma,
@@ -442,7 +464,7 @@
                 dma, dma((2,)),
                 dma, dma((REUSE_Y,)), dma, dma((REUSE_X + 1,)),
                 dma, dma((chunks // 2,)),
-                dma, dma, dma, dma((4, 2)), dma, dma,
+                dma, dma, dma, dma((6,)), dma((3,)), dma,
                 pltpu.SemaphoreType.REGULAR((2,)),
             ],
             compiler_params=pltpu.CompilerParams(collective_id=0, has_side_effects=True, vmem_limit_bytes=60 * 2**20),

time: 76.2 us -> 78.2 us (1.026)
  Pallas kernels: 74.8 us -> 76.5 us
    pallas_call x1, Pallas kernels: 74 us -> 75.8 us  [local_search(): pl.pallas_call(functools.partial(search_kernel, dims), out_shape=pltpu.VM...]
where the time goes in v13:
time: 78.2 us; the launch traced here: 77.2 us
  Pallas kernels  76.5 us (98%)
    pallas_call x1, Pallas kernels, local_search(): pl.pallas_call(functools.partial(search_kernel, dims), out_shape=pltpu.VM...  75.8 us

profile of v13, /device:TPU:0, one launch (start us, length us, event | category | flops | bytes accessed | tf_op | source)
XLA Modules:
  0.0 77.2 jit_solution(5788362173881418969)
XLA Ops:
  0.6 75.8 %ivf_search.1.res = f32[8,40,128]{2,1,0:T(8,128)S(1)} custom-call(bf16[2048,1024]{1,0:T(8,128)(2,1)} %q_hbm.1, bf16[2048,1024]{1,0:T(8,128)(2,1)} %bitcast.5, s32[8,2048]{1,0:T(8,128)} %bitcast.6, s32[8,256]{1,0:T(8,128)} %bitcast.7), custom_call_target="tpu_custom_call" | custom-call | tf_op jit(solution)/shard_map/ivf_search/pallas_call | solution.py:446
  76.4 0.7 place.1

commit v14 on v12

--- a/solution.py
+++ b/solution.py
@@ -24,8 +24,8 @@
     return index + bit - 2 * bit * ((index // bit) % 2)
 
 
-def search_kernel(dims, q_hbm, l_hbm, probes_hbm, ids_hbm, res,
-                  raw, qv, vecs, perm, acc, parts, ids_all, cand_ids, probes_ref, ids_ref, load_p, load_i,
+def search_kernel(dims, q_hbm, l_hbm, probes_hbm, ids_hbm, res, kept_hbm,
+                  raw, qv, vecs, perm, acc, parts, ids_all, cand_ids, probes_ref, ids_ref, load_p, load_i, keep_sem,
                   load_l, load_q, send_o, recv_o, send_y, recv_y, send_x, recv_x,
                   send_d, recv_d, send_i, recv_i, send_r, recv_r, send_g, recv_g, met):
     rows_q = qv.shape[0]
@@ -74,17 +74,47 @@
     def slot(chunk, which):
         return piece(2 * block_groups + STEP_GROUPS * (chunk // 2) + which, chunk)
 
-    def y_copy(chunk):
-        return remote(piece(chunks // 2 * x + chunk // 2, chunk), slot(chunk, 0), send_y, recv_y.at[chunk % REUSE_Y], at(shard=across))
+    early_chunks = STEP_ROWS // PIECE_ROWS
+
+    def y_copy(chunk, source=None):
+        source = piece(chunks // 2 * x + chunk // 2, chunk) if source is None else source
+        return remote(source, slot(chunk, 0), send_y, recv_y.at[chunk % REUSE_Y], at(shard=across))
+
+    def y_send(chunk):
+        @pl.when(chunk < early_chunks)
+        def _():
+            y_copy(chunk).start()
+
+        @pl.when((chunk >= early_chunks) & (chunk < chunks))
+        def _():
+            y_copy(chunk, kept_hbm.at[pl.ds(pl.multiple_of(chunk * PIECE_ROWS, PIECE_ROWS), PIECE_ROWS)]).start()
+
+    def keep(turn):
+        rows = pl.ds(pl.multiple_of(turn * STEP_ROWS, STEP_ROWS), STEP_ROWS)
+        return pltpu.make_async_copy(vecs.at[step_rows(block_at(turn))], kept_hbm.at[rows], keep_sem)
 
     def x_copy(chunk):
         return remote(slot(chunk, 0), slot(chunk, 1), send_x, recv_x.at[chunk % REUSE_X], at(rep=other_x))
 
-    def dy_copy(chunk):
-        return remote(slot(chunk, 0), slot(chunk, 2), send_d, recv_d.at[chunk // 2], at(shard=twin))
-
-    def dx_copy(chunk):
-        return remote(slot(chunk, 1), slot(chunk, 3), send_d, recv_d.at[chunk // 2], at(shard=twin))
+    def whole(group, which):
+        return vecs.at[pl.ds(pl.multiple_of((2 * block_groups + STEP_GROUPS * group + which) * GROUP_ROWS, GROUP_ROWS), GROUP_ROWS)]
+
+    def twin_copy(group, which):
+        return remote(whole(group, which), whole(group, which + 2), send_d, recv_d.at[group], at(shard=twin))
+
+    def twin_piece(chunk, which):
+        return remote(slot(chunk, which), slot(chunk, which + 2), send_d, recv_d.at[chunk // 2], at(shard=twin))
+
+    def pair_up(chunk, which):
+        if isinstance(chunk, int):
+            if which == 1 and chunk // 2 == chunks // 2 - 1:
+                twin_piece(chunk, which).start()
+            elif chunk % 2 == 1:
+                twin_copy(chunk // 2, which).start()
+        else:
+            @pl.when(chunk % 2 == 1)
+            def _():
+                twin_copy(chunk // 2, which).start()
 
     def id_copy(which, peer):
         return remote(ids_ref, ids_all.at[s], send_i, recv_i, at(shard=peer))
@@ -222,11 +252,8 @@
         y_copy(chunk).wait_recv()
         if not (isinstance(chunk, int) and chunk == chunks - 1):
             x_copy(chunk).start()
-        dy_copy(chunk).start()
-
-        @pl.when(chunk + window < chunks)
-        def _():
-            y_copy(chunk + window).start()
+        pair_up(chunk, 0)
+        y_send(chunk + window)
 
         @pl.when(chunk + window == chunks)
         def _():
@@ -237,7 +264,7 @@
             spare_copy.wait_recv()
         else:
             x_copy(chunk).wait_recv()
-        dx_copy(chunk).start()
+        pair_up(chunk, 1)
 
     def await_step(step):
         await_recv(vecs.at[pl.ds(0, 4 * PIECE_ROWS)], recv_d.at[step - 2 * block_steps])
@@ -249,6 +276,15 @@
 
     def early(step, carry):
         own_copy(block_at(step)).start()
+        half = block_steps // 2
+
+        @pl.when((step >= 2) & (step <= half))
+        def _():
+            keep(step - 1).wait()
+
+        @pl.when((step >= 1) & (step < half))
+        def _():
+            keep(step).start()
 
         @pl.when(step >= 1)
         def _():
@@ -421,11 +457,12 @@
         dma = pltpu.SemaphoreType.DMA
         any_spec = pl.BlockSpec(memory_space=pl.ANY)
         vmem_spec = pl.BlockSpec(memory_space=pltpu.VMEM)
-        found = pl.pallas_call(
+        found, _ = pl.pallas_call(
             functools.partial(search_kernel, dims),
-            out_shape=pltpu.VMEM((dims, 2, TOP_K * width // LANES, LANES), jnp.float32),
+            out_shape=(pltpu.VMEM((dims, 2, TOP_K * width // LANES, LANES), jnp.float32),
+                       jax.ShapeDtypeStruct((block_rows // 2, depth), jnp.bfloat16)),
             in_specs=[any_spec] * 4,
-            out_specs=vmem_spec,
+            out_specs=(vmem_spec, any_spec),
             scratch_shapes=[
                 pltpu.VMEM((block_rows, depth), jnp.bfloat16),
                 pltpu.VMEM((rows_q, depth), jnp.bfloat16),
@@ -437,7 +474,7 @@
                 pltpu.VMEM((2, LIST_LEN, probe_count, width // 2), jnp.float32),
                 pltpu.VMEM((probe_count, rows_q), jnp.int32),
                 pltpu.VMEM((LIST_LEN, lists_dev), jnp.int32),
-                dma, dma,
+                dma, dma, dma,
                 dma((3,)), dma,
                 dma, dma((2,)),
                 dma, dma((REUSE_Y,)), dma, dma((REUSE_X + 1,)),

time: 76.2 us -> 76.7 us (level)
  no operation moved by 1% of the time
where the time goes in v14:
time: 76.7 us; the launch traced here: 75.8 us
  Pallas kernels  75.2 us (98%)
    pallas_call x1, Pallas kernels, local_search(): pl.pallas_call(functools.partial(search_kernel, dims), out_shape=(pltpu.V...  74.5 us

profile of v14, /device:TPU:0, one launch (start us, length us, event | category | flops | bytes accessed | tf_op | source)
XLA Modules:
  0.0 75.8 jit_solution(14727250699272924260)
XLA Ops:
  0.6 74.5 %ivf_search.1 = (f32[4,2,40,128]{3,2,1,0:T(8,128)S(1)}, bf16[1024,1024]{1,0:T(8,128)(2,1)}) custom-call(bf16[2048,1024]{1,0:T(8,128)(2,1)} %q_hbm.1, bf16[2048,1024]{1,0:T(8,128)(2,1)} %bitcast.5, s32[8,2048]{1,0:T(8,128)} %bitcast.6, s32[8,256]{1,0:T(8,128)} %bitcast.7), custom_call_target="tpu_custom_call" | custom-call | tf_op jit(solution)/shard_map/ivf_search/pallas_call | solution.py:460
  75.1 0.7 place.1

commit v15 on v12

--- a/solution.py
+++ b/solution.py
@@ -80,11 +80,25 @@
     def x_copy(chunk):
         return remote(slot(chunk, 0), slot(chunk, 1), send_x, recv_x.at[chunk % REUSE_X], at(rep=other_x))
 
-    def dy_copy(chunk):
-        return remote(slot(chunk, 0), slot(chunk, 2), send_d, recv_d.at[chunk // 2], at(shard=twin))
-
-    def dx_copy(chunk):
-        return remote(slot(chunk, 1), slot(chunk, 3), send_d, recv_d.at[chunk // 2], at(shard=twin))
+    def whole(group, which):
+        return vecs.at[pl.ds(pl.multiple_of((2 * block_groups + STEP_GROUPS * group + which) * GROUP_ROWS, GROUP_ROWS), GROUP_ROWS)]
+
+    def twin_copy(group, which):
+        return remote(whole(group, which), whole(group, which + 2), send_d, recv_d.at[group], at(shard=twin))
+
+    def twin_piece(chunk, which):
+        return remote(slot(chunk, which), slot(chunk, which + 2), send_d, recv_d.at[chunk // 2], at(shard=twin))
+
+    def pair_up(chunk, which):
+        if isinstance(chunk, int):
+            if which == 1 and chunk // 2 == chunks // 2 - 1:
+                twin_piece(chunk, which).start()
+            elif chunk % 2 == 1:
+                twin_copy(chunk // 2, which).start()
+        else:
+            @pl.when(chunk % 2 == 1)
+            def _():
+                twin_copy(chunk // 2, which).start()
 
     def id_copy(which, peer):
         return remote(ids_ref, ids_all.at[s], send_i, recv_i, at(shard=peer))
@@ -222,7 +236,7 @@
         y_copy(chunk).wait_recv()
         if not (isinstance(chunk, int) and chunk == chunks - 1):
             x_copy(chunk).start()
-        dy_copy(chunk).start()
+        pair_up(chunk, 0)
 
         @pl.when(chunk + window < chunks)
         def _():
@@ -237,7 +251,7 @@
             spare_copy.wait_recv()
         else:
             x_copy(chunk).wait_recv()
-        dx_copy(chunk).start()
+        pair_up(chunk, 1)
 
     def await_step(step):
         await_recv(vecs.at[pl.ds(0, 4 * PIECE_ROWS)], recv_d.at[step - 2 * block_steps])

time: 76.2 us -> 76.6 us (level)
  no operation moved by 1% of the time
where the time goes in v15:
time: 76.6 us; the launch traced here: 75.8 us
  Pallas kernels  75.1 us (98%)
    pallas_call x1, Pallas kernels, local_search(): pl.pallas_call(functools.partial(search_kernel, dims), out_shape=pltpu.VM...  74.4 us

profile of v15, /device:TPU:0, one launch (start us, length us, event | category | flops | bytes accessed | tf_op | source)
XLA Modules:
  0.0 75.8 jit_solution(3650233635623748223)
XLA Ops:
  0.6 74.4 %ivf_search.1.res = f32[4,2,40,128]{3,2,1,0:T(8,128)S(1)} custom-call(bf16[2048,1024]{1,0:T(8,128)(2,1)} %q_hbm.1, bf16[2048,1024]{1,0:T(8,128)(2,1)} %bitcast.5, s32[8,2048]{1,0:T(8,128)} %bitcast.6, s32[8,256]{1,0:T(8,128)} %bitcast.7), custom_call_target="tpu_custom_call" | custom-call | tf_op jit(solution)/shard_map/ivf_search/pallas_call | solution.py:438
  75.0 0.7 place.1

commit v16 on v12

--- a/solution.py
+++ b/solution.py
@@ -93,15 +93,25 @@
     mate, far_outer = flip(z, 1), jnp.where(z < 2, dims - 1, 0)
     far_inner = flip(far_outer, 1)
 
-    def part_copy(target, place, half):
-        return remote(acc.at[target, half], parts.at[place, half], send_r, recv_r.at[place, half], at(dim=mate))
-
-    def merged_copy(merge, half):
-        return remote(parts.at[merge, half], parts.at[3, half], send_r, recv_r.at[3, half],
-                      at(dim=(far_outer, far_inner)[merge]))
-
-    def part_wait(place, half):
-        await_recv(parts.at[place, half], recv_r.at[place, half])
+    def landed(place, half, sub=0):
+        return recv_r.at[12 + half if place == 2 else 4 * min(place, 2) + 2 * half + sub]
+
+    def some_members(sub):
+        return pl.ds(sub * (LIST_LEN // 2), LIST_LEN // 2)
+
+    def near_copy(half):
+        return remote(acc.at[mate, half], parts.at[2, half], send_r, landed(2, half), at(dim=mate))
+
+    def cross_copy(target, place, half, sub):
+        return remote(acc.at[target, half, some_members(sub)], parts.at[place, half, some_members(sub)], send_r,
+                      landed(place, half, sub), at(dim=mate))
+
+    def merged_copy(merge, half, sub):
+        return remote(parts.at[merge, half, some_members(sub)], parts.at[3, half, some_members(sub)], send_r,
+                      landed(3, half, sub), at(dim=(far_outer, far_inner)[merge]))
+
+    def part_wait(place, half, sub):
+        await_recv(parts.at[place, half, some_members(sub)], landed(place, half, sub))
 
     def res_copy(target, half):
         return remote(res.at[z, half], res.at[z, half], send_g, recv_g, at(dim=target))
@@ -321,21 +331,31 @@
 
     leads, follows = outer & (s % 2 == 0), outer & (s % 2 == 1)
 
+    def send_cross(*plan):
+        for far_place, half in plan:
+            for sub in range(2):
+                cross_copy((far_outer, far_inner)[far_place], far_place, half, sub).start()
+
+    def send_near():
+        for half in range(2):
+            near_copy(half).start()
+
     def finish(turn, carry):
         @pl.when(leads & (turn == 1))
         def _():
-            part_copy(far_outer, 0, 0).start()
+            send_cross((0, 0))
 
         @pl.when(leads & (turn == 2))
         def _():
-            part_copy(far_inner, 1, 0).start()
-            part_copy(far_outer, 0, 1).start()
-            part_copy(far_inner, 1, 1).start()
+            send_cross((1, 0), (0, 1), (1, 1))
+
+        @pl.when(follows & (turn == 3))
+        def _():
+            send_cross((0, 0), (1, 0))
 
         @pl.when((leads & (turn == 3)) | (jnp.logical_not(outer) & (turn == 1)))
         def _():
-            for half in range(2):
-                part_copy(mate, 2, half).start()
+            send_near()
         score(jnp.int32(last), last_heads, target_at(turn))
         return carry
 
@@ -343,24 +363,23 @@
 
     @pl.when(follows)
     def _():
-        for half in range(2):
-            part_copy(far_outer, 0, half).start()
-            part_copy(far_inner, 1, half).start()
-        for half in range(2):
-            part_copy(mate, 2, half).start()
+        send_cross((0, 1), (1, 1))
+        send_near()
 
     @pl.when(jnp.logical_not(outer))
     def _():
         for half in range(2):
             for merge, target in enumerate((far_outer, far_inner)):
-                part_wait(merge, half)
-                parts[merge, half] += acc[target, half]
-                merged_copy(merge, half).start()
+                for sub in range(2):
+                    part_wait(merge, half, sub)
+                    parts[merge, half, some_members(sub)] += acc[target, half, some_members(sub)]
+                    merged_copy(merge, half, sub).start()
 
     tiles = width // 2 // LANES
     for half in range(2):
-        part_wait(2, half)
-        part_wait(3, half)
+        await_recv(parts.at[2, half], landed(2, half))
+        for sub in range(2):
+            part_wait(3, half, sub)
         scores, names = [], []
         for member in range(LIST_LEN):
             total = acc[z, half, member] + parts[2, half, member] + parts[3, half, member]
@@ -442,7 +461,7 @@
                 dma, dma((2,)),
                 dma, dma((REUSE_Y,)), dma, dma((REUSE_X + 1,)),
                 dma, dma((chunks // 2,)),
-                dma, dma, dma, dma((4, 2)), dma, dma,
+                dma, dma, dma, dma((14,)), dma, dma,
                 pltpu.SemaphoreType.REGULAR((2,)),
             ],
             compiler_params=pltpu.CompilerParams(collective_id=0, has_side_effects=True, vmem_limit_bytes=60 * 2**20),

time: 76.2 us -> 75.5 us (level)
  no operation moved by 1% of the time
where the time goes in v16:
time: 75.5 us; the launch traced here: 75.4 us
  Pallas kernels  74.7 us (99%)
    pallas_call x1, Pallas kernels, local_search(): pl.pallas_call(functools.partial(search_kernel, dims), out_shape=pltpu.VM...  74 us

profile of v16, /device:TPU:0, one launch (start us, length us, event | category | flops | bytes accessed | tf_op | source)
XLA Modules:
  0.0 75.4 jit_solution(16515373609043871647)
XLA Ops:
  0.6 74.0 %ivf_search.1.res = f32[4,2,40,128]{3,2,1,0:T(8,128)S(1)} custom-call(bf16[2048,1024]{1,0:T(8,128)(2,1)} %q_hbm.1, bf16[2048,1024]{1,0:T(8,128)(2,1)} %bitcast.5, s32[8,2048]{1,0:T(8,128)} %bitcast.6, s32[8,256]{1,0:T(8,128)} %bitcast.7), custom_call_target="tpu_custom_call" | custom-call | tf_op jit(solution)/shard_map/ivf_search/pallas_call | solution.py:443
  74.7 0.7 place.1

commit v17 on v16

--- a/solution.py
+++ b/solution.py
@@ -63,9 +63,11 @@
 
     queries_in = pltpu.make_async_copy(q_hbm, qv, load_q)
 
-    def own_copy(block):
-        return remote(vecs.at[step_rows(block)], vecs.at[step_rows(block_steps + block)],
-                      send_o, recv_o.at[(block // (block_steps // 2) + x) % 2], at(shard=twin))
+    def send_own(block):
+        for part in range(STEP_ROWS // PIECE_ROWS):
+            first = pl.multiple_of(block * STEP_ROWS + part * PIECE_ROWS, PIECE_ROWS)
+            remote(vecs.at[pl.ds(first, PIECE_ROWS)], vecs.at[pl.ds(block_rows + first, PIECE_ROWS)],
+                   send_o, recv_o.at[(block // (block_steps // 2) + x) % 2], at(shard=twin)).start()
 
     def piece(group, chunk):
         first = pl.multiple_of(group * GROUP_ROWS + chunk % 2 * PIECE_ROWS, PIECE_ROWS)
@@ -258,7 +260,7 @@
             score(step, heads, part)
 
     def early(step, carry):
-        own_copy(block_at(step)).start()
+        send_own(block_at(step))
 
         @pl.when(step >= 1)
         def _():
@@ -285,7 +287,7 @@
 
         @pl.when(step == block_steps - 1)
         def _():
-            own_copy(block_at(step)).start()
+            send_own(block_at(step))
 
         @pl.when((step == block_steps) | (step == block_steps + block_steps // 2))
         def _():

time: 75.5 us -> 75.5 us (level)
  no operation moved by 1% of the time
where the time goes in v17:
time: 75.5 us; the launch traced here: 75.4 us
  Pallas kernels  74.7 us (99%)
    pallas_call x1, Pallas kernels, local_search(): pl.pallas_call(functools.partial(search_kernel, dims), out_shape=pltpu.VM...  74 us

profile of v17, /device:TPU:0, one launch (start us, length us, event | category | flops | bytes accessed | tf_op | source)
XLA Modules:
  0.0 75.4 jit_solution(2090402669448806873)
XLA Ops:
  0.6 74.0 %ivf_search.1.res = f32[4,2,40,128]{3,2,1,0:T(8,128)S(1)} custom-call(bf16[2048,1024]{1,0:T(8,128)(2,1)} %q_hbm.1, bf16[2048,1024]{1,0:T(8,128)(2,1)} %bitcast.5, s32[8,2048]{1,0:T(8,128)} %bitcast.6, s32[8,256]{1,0:T(8,128)} %bitcast.7), custom_call_target="tpu_custom_call" | custom-call | tf_op jit(solution)/shard_map/ivf_search/pallas_call | solution.py:445
  74.7 0.7 place.1

commit v18 on v16

--- a/solution.py
+++ b/solution.py
@@ -228,15 +228,45 @@
     spare_copy = remote(piece(chunks // 2 * other_x + (chunks - 1) // 2, chunks - 1), slot(chunks - 1, 1),
                         send_x, recv_x.at[REUSE_X], at(shard=across))
 
+    split = chunks - 2
+
+    def split_half(buffer, half):
+        return buffer.at[pl.ds(half * (PIECE_ROWS // 2), PIECE_ROWS // 2)]
+
+    def y_half(half):
+        return remote(split_half(piece(chunks // 2 * x + split // 2, split), half), split_half(slot(split, 0), half),
+                      send_y, recv_y.at[REUSE_Y + half], at(shard=across))
+
+    def x_half(half):
+        return remote(split_half(slot(split, 0), half), split_half(slot(split, 1), half),
+                      send_x, recv_x.at[REUSE_X + 1 + half], at(rep=other_x))
+
+    def d_half(which, half):
+        return remote(split_half(slot(split, which), half), split_half(slot(split, which + 2), half),
+                      send_d, recv_d.at[split // 2], at(shard=twin))
+
+    def pass_split(which):
+        for half in range(2):
+            if which == 0:
+                y_half(half).wait_recv()
+                x_half(half).start()
+            else:
+                x_half(half).wait_recv()
+            d_half(which, half).start()
+
     def pass_y(chunk):
         y_copy(chunk).wait_recv()
         if not (isinstance(chunk, int) and chunk == chunks - 1):
             x_copy(chunk).start()
         dy_copy(chunk).start()
 
-        @pl.when(chunk + window < chunks)
-        def _():
-            y_copy(chunk + window).start()
+        if isinstance(chunk, int) and chunk + window == split:
+            for half in range(2):
+                y_half(half).start()
+        else:
+            @pl.when(chunk + window < chunks)
+            def _():
+                y_copy(chunk + window).start()
 
         @pl.when(chunk + window == chunks)
         def _():
@@ -314,7 +344,11 @@
                         await_recv(ids_all.at[pl.ds(0, 3)], recv_i)
                         lax.fori_loop(0, width // LANES, name_candidates, 0)
                     else:
-                        (pass_y if word[0] == 'y' else pass_x)(int(word[1:]))
+                        which, number = 'yx'.index(word[0]), int(word[1:])
+                        if number == split:
+                            pass_split(which)
+                        else:
+                            (pass_y, pass_x)[which](number)
 
         await_step(step)
         score_all(step)
@@ -459,7 +493,7 @@
                 dma, dma,
                 dma((3,)), dma,
                 dma, dma((2,)),
-                dma, dma((REUSE_Y,)), dma, dma((REUSE_X + 1,)),
+                dma, dma((REUSE_Y + 2,)), dma, dma((REUSE_X + 3,)),
                 dma, dma((chunks // 2,)),
                 dma, dma, dma, dma((14,)), dma, dma,
                 pltpu.SemaphoreType.REGULAR((2,)),

time: 75.5 us -> 75.5 us (level)
  no operation moved by 1% of the time
where the time goes in v18:
time: 75.5 us; the launch traced here: 75.3 us
  Pallas kernels  74.7 us (99%)
    pallas_call x1, Pallas kernels, local_search(): pl.pallas_call(functools.partial(search_kernel, dims), out_shape=pltpu.VM...  74 us

profile of v18, /device:TPU:0, one launch (start us, length us, event | category | flops | bytes accessed | tf_op | source)
XLA Modules:
  0.0 75.3 jit_solution(7094473995178422014)
XLA Ops:
  0.6 74.0 %ivf_search.1.res = f32[4,2,40,128]{3,2,1,0:T(8,128)S(1)} custom-call(bf16[2048,1024]{1,0:T(8,128)(2,1)} %q_hbm.1, bf16[2048,1024]{1,0:T(8,128)(2,1)} %bitcast.5, s32[8,2048]{1,0:T(8,128)} %bitcast.6, s32[8,256]{1,0:T(8,128)} %bitcast.7), custom_call_target="tpu_custom_call" | custom-call | tf_op jit(solution)/shard_map/ivf_search/pallas_call | solution.py:477
  74.6 0.7 place.1

commit v19 on v18

--- a/solution.py
+++ b/solution.py
@@ -441,7 +441,7 @@
             await_send(vecs.at[pl.ds(0, chunks * PIECE_ROWS)], send_x)
             await_send(vecs.at[pl.ds(0, 2 * chunks * PIECE_ROWS)], send_d)
         for which in range(dims - 1):
-            res_copy(target_at(which), half).start()
+            res_copy(jnp.where(which < z, which, which + 1), half).start()
 
     await_send(parts.at[pl.ds(0, 3)], send_r)
     await_send(res.at[pl.ds(0, dims - 1)], send_g)

time: 75.5 us -> 75.5 us (level)
  no operation moved by 1% of the time
where the time goes in v19:
time: 75.5 us; the launch traced here: 75.3 us
  Pallas kernels  74.7 us (99%)
    pallas_call x1, Pallas kernels, local_search(): pl.pallas_call(functools.partial(search_kernel, dims), out_shape=pltpu.VM...  74 us

profile of v19, /device:TPU:0, one launch (start us, length us, event | category | flops | bytes accessed | tf_op | source)
XLA Modules:
  0.0 75.3 jit_solution(3343982435255873289)
XLA Ops:
  0.6 74.0 %ivf_search.1.res = f32[4,2,40,128]{3,2,1,0:T(8,128)S(1)} custom-call(bf16[2048,1024]{1,0:T(8,128)(2,1)} %q_hbm.1, bf16[2048,1024]{1,0:T(8,128)(2,1)} %bitcast.5, s32[8,2048]{1,0:T(8,128)} %bitcast.6, s32[8,256]{1,0:T(8,128)} %bitcast.7), custom_call_target="tpu_custom_call" | custom-call | tf_op jit(solution)/shard_map/ivf_search/pallas_call | solution.py:477
  74.6 0.7 place.1

commit v20 on v19

--- a/solution.py
+++ b/solution.py
@@ -117,7 +117,7 @@
         return remote(res.at[z, half], res.at[z, half], send_g, recv_g, at(dim=target))
 
     def target_at(turn):
-        first, second, third = (jnp.where(outer, one, two) for one, two in ((far_outer, mate), (far_inner, far_outer), (mate, far_inner)))
+        first, second, third = (jnp.where(outer, one, two) for one, two in ((far_inner, mate), (far_outer, far_inner), (mate, far_outer)))
         return jnp.where(turn == 0, first, jnp.where(turn == 1, second, jnp.where(turn == 2, third, z)))
 
     def block_at(turn):
@@ -377,15 +377,15 @@
     def finish(turn, carry):
         @pl.when(leads & (turn == 1))
         def _():
-            send_cross((0, 0))
+            send_cross((1, 0))
 
         @pl.when(leads & (turn == 2))
         def _():
-            send_cross((1, 0), (0, 1), (1, 1))
+            send_cross((0, 0), (1, 1), (0, 1))
 
         @pl.when(follows & (turn == 3))
         def _():
-            send_cross((0, 0), (1, 0))
+            send_cross((1, 0), (0, 0))
 
         @pl.when((leads & (turn == 3)) | (jnp.logical_not(outer) & (turn == 1)))
         def _():
@@ -397,13 +397,13 @@
 
     @pl.when(follows)
     def _():
-        send_cross((0, 1), (1, 1))
+        send_cross((1, 1), (0, 1))
         send_near()
 
     @pl.when(jnp.logical_not(outer))
     def _():
         for half in range(2):
-            for merge, target in enumerate((far_outer, far_inner)):
+            for merge, target in ((1, far_inner), (0, far_outer)):
                 for sub in range(2):
                     part_wait(merge, half, sub)
                     parts[merge, half, some_members(sub)] += acc[target, half, some_members(sub)]

time: 75.5 us -> 75.4 us (level)
  no operation moved by 1% of the time
where the time goes in v20:
time: 75.4 us; the launch traced here: 75.2 us
  Pallas kernels  74.6 us (99%)
    pallas_call x1, Pallas kernels, local_search(): pl.pallas_call(functools.partial(search_kernel, dims), out_shape=pltpu.VM...  73.9 us

profile of v20, /device:TPU:0, one launch (start us, length us, event | category | flops | bytes accessed | tf_op | source)
XLA Modules:
  0.0 75.2 jit_solution(4841785521724168465)
XLA Ops:
  0.6 73.9 %ivf_search.1.res = f32[4,2,40,128]{3,2,1,0:T(8,128)S(1)} custom-call(bf16[2048,1024]{1,0:T(8,128)(2,1)} %q_hbm.1, bf16[2048,1024]{1,0:T(8,128)(2,1)} %bitcast.5, s32[8,2048]{1,0:T(8,128)} %bitcast.6, s32[8,256]{1,0:T(8,128)} %bitcast.7), custom_call_target="tpu_custom_call" | custom-call | tf_op jit(solution)/shard_map/ivf_search/pallas_call | solution.py:477
  74.5 0.7 place.1

commit v21 on v20

--- a/solution.py
+++ b/solution.py
@@ -381,7 +381,7 @@
 
         @pl.when(leads & (turn == 2))
         def _():
-            send_cross((0, 0), (1, 1), (0, 1))
+            send_cross((0, 0))
 
         @pl.when(follows & (turn == 3))
         def _():
@@ -390,6 +390,10 @@
         @pl.when((leads & (turn == 3)) | (jnp.logical_not(outer) & (turn == 1)))
         def _():
             send_near()
+
+        @pl.when(leads & (turn == 3))
+        def _():
+            send_cross((1, 1), (0, 1))
         score(jnp.int32(last), last_heads, target_at(turn))
         return carry
 
@@ -397,8 +401,8 @@
 
     @pl.when(follows)
     def _():
+        send_near()
         send_cross((1, 1), (0, 1))
-        send_near()
 
     @pl.when(jnp.logical_not(outer))
     def _():

time: 75.4 us -> 78.6 us (1.042)
  Pallas kernels: 74.6 us -> 77.8 us
    pallas_call x1, Pallas kernels: 73.9 us -> 77 us  [local_search(): pl.pallas_call(functools.partial(search_kernel, dims), out_shape=pltpu.VM...]
where the time goes in v21:
time: 78.6 us; the launch traced here: 78.4 us
  Pallas kernels  77.8 us (99%)
    pallas_call x1, Pallas kernels, local_search(): pl.pallas_call(functools.partial(search_kernel, dims), out_shape=pltpu.VM...  77 us

profile of v21, /device:TPU:0, one launch (start us, length us, event | category | flops | bytes accessed | tf_op | source)
XLA Modules:
  0.0 78.4 jit_solution(3402556694733509996)
XLA Ops:
  0.6 77.0 %ivf_search.1.res = f32[4,2,40,128]{3,2,1,0:T(8,128)S(1)} custom-call(bf16[2048,1024]{1,0:T(8,128)(2,1)} %q_hbm.1, bf16[2048,1024]{1,0:T(8,128)(2,1)} %bitcast.5, s32[8,2048]{1,0:T(8,128)} %bitcast.6, s32[8,256]{1,0:T(8,128)} %bitcast.7), custom_call_target="tpu_custom_call" | custom-call | tf_op jit(solution)/shard_map/ivf_search/pallas_call | solution.py:481
  77.7 0.7 place.1

commit v22 on v20

--- a/solution.py
+++ b/solution.py
@@ -16,6 +16,7 @@
 PIECE_ROWS = GROUP_ROWS // 2
 LANES = 128
 REUSE_Y, REUSE_X = 8, 12
+SUBS = 4
 MESH = pl.DeviceIdType.MESH
 BIG = 1e9
 
@@ -94,10 +95,10 @@
     far_inner = flip(far_outer, 1)
 
     def landed(place, half, sub=0):
-        return recv_r.at[12 + half if place == 2 else 4 * min(place, 2) + 2 * half + sub]
+        return recv_r.at[6 * SUBS + half if place == 2 else (2 * min(place, 2) + half) * SUBS + sub]
 
     def some_members(sub):
-        return pl.ds(sub * (LIST_LEN // 2), LIST_LEN // 2)
+        return pl.ds(sub * (LIST_LEN // SUBS), LIST_LEN // SUBS)
 
     def near_copy(half):
         return remote(acc.at[mate, half], parts.at[2, half], send_r, landed(2, half), at(dim=mate))
@@ -367,7 +368,7 @@
 
     def send_cross(*plan):
         for far_place, half in plan:
-            for sub in range(2):
+            for sub in range(SUBS):
                 cross_copy((far_outer, far_inner)[far_place], far_place, half, sub).start()
 
     def send_near():
@@ -404,7 +405,7 @@
     def _():
         for half in range(2):
             for merge, target in ((1, far_inner), (0, far_outer)):
-                for sub in range(2):
+                for sub in range(SUBS):
                     part_wait(merge, half, sub)
                     parts[merge, half, some_members(sub)] += acc[target, half, some_members(sub)]
                     merged_copy(merge, half, sub).start()
@@ -412,7 +413,7 @@
     tiles = width // 2 // LANES
     for half in range(2):
         await_recv(parts.at[2, half], landed(2, half))
-        for sub in range(2):
+        for sub in range(SUBS):
             part_wait(3, half, sub)
         scores, names = [], []
         for member in range(LIST_LEN):
@@ -495,7 +496,7 @@
                 dma, dma((2,)),
                 dma, dma((REUSE_Y + 2,)), dma, dma((REUSE_X + 3,)),
                 dma, dma((chunks // 2,)),
-                dma, dma, dma, dma((14,)), dma, dma,
+                dma, dma, dma, dma((6 * SUBS + 2,)), dma, dma,
                 pltpu.SemaphoreType.REGULAR((2,)),
             ],
             compiler_params=pltpu.CompilerParams(collective_id=0, has_side_effects=True, vmem_limit_bytes=60 * 2**20),

time: 75.4 us -> 75.5 us (level)
  no operation moved by 1% of the time
where the time goes in v22:
time: 75.5 us; the launch traced here: 75.3 us
  Pallas kernels  74.7 us (99%)
    pallas_call x1, Pallas kernels, local_search(): pl.pallas_call(functools.partial(search_kernel, dims), out_shape=pltpu.VM...  74 us

profile of v22, /device:TPU:0, one launch (start us, length us, event | category | flops | bytes accessed | tf_op | source)
XLA Modules:
  0.0 75.3 jit_solution(4992206737099803944)
XLA Ops:
  0.6 74.0 %ivf_search.1.res = f32[4,2,40,128]{3,2,1,0:T(8,128)S(1)} custom-call(bf16[2048,1024]{1,0:T(8,128)(2,1)} %q_hbm.1, bf16[2048,1024]{1,0:T(8,128)(2,1)} %bitcast.5, s32[8,2048]{1,0:T(8,128)} %bitcast.6, s32[8,256]{1,0:T(8,128)} %bitcast.7), custom_call_target="tpu_custom_call" | custom-call | tf_op jit(solution)/shard_map/ivf_search/pallas_call | solution.py:478
  74.6 0.7 place.1

commit v23 on v20

--- a/solution.py
+++ b/solution.py
@@ -383,9 +383,13 @@
         def _():
             send_cross((0, 0), (1, 1), (0, 1))
 
+        @pl.when(follows & (turn == 2))
+        def _():
+            send_cross((1, 0))
+
         @pl.when(follows & (turn == 3))
         def _():
-            send_cross((1, 0), (0, 0))
+            send_cross((0, 0))
 
         @pl.when((leads & (turn == 3)) | (jnp.logical_not(outer) & (turn == 1)))
         def _():

time: 75.4 us -> 75.7 us (level)
  no operation moved by 1% of the time
where the time goes in v23:
time: 75.7 us; the launch traced here: 75.5 us
  Pallas kernels  74.9 us (99%)
    pallas_call x1, Pallas kernels, local_search(): pl.pallas_call(functools.partial(search_kernel, dims), out_shape=pltpu.VM...  74.2 us

profile of v23, /device:TPU:0, one launch (start us, length us, event | category | flops | bytes accessed | tf_op | source)
XLA Modules:
  0.0 75.5 jit_solution(6133993119814799152)
XLA Ops:
  0.6 74.2 %ivf_search.1.res = f32[4,2,40,128]{3,2,1,0:T(8,128)S(1)} custom-call(bf16[2048,1024]{1,0:T(8,128)(2,1)} %q_hbm.1, bf16[2048,1024]{1,0:T(8,128)(2,1)} %bitcast.5, s32[8,2048]{1,0:T(8,128)} %bitcast.6, s32[8,256]{1,0:T(8,128)} %bitcast.7), custom_call_target="tpu_custom_call" | custom-call | tf_op jit(solution)/shard_map/ivf_search/pallas_call | solution.py:481
  74.8 0.7 place.1
